TPU v7x, 128 devices: a whole 4x4x4 slice. The times are simulated.
128 devices in a mesh: tp: 2 (over core), dp: 64 (over z, y, x).
Axes of the slice: x: 4, y: 4, z: 4, core: 2. Of those that a mesh axis runs over, the one named last changes fastest.
Arguments:
- hidden: bfloat16 [128, 64, 3072], P('dp')
- positions: int32 [64], replicated
- ln1_gain: bfloat16 [3072], replicated
- ln1_bias: bfloat16 [3072], replicated
- w_q: bfloat16 [3072, 3072], P(None, 'tp')
- w_k: bfloat16 [3072, 1024], P(None, 'tp')
- w_v: bfloat16 [3072, 1024], P(None, 'tp')
- w_o: bfloat16 [3072, 3072], P('tp')
- ln2_gain: bfloat16 [3072], replicated
- ln2_bias: bfloat16 [3072], replicated
- w_up: bfloat16 [3072, 9216], P(None, 'tp')
- w_down: bfloat16 [9216, 3072], P('tp')
Outputs:
- output 1: bfloat16 [128, 64, 3072], P('dp')
- output 2: float32 [9216], P('tp')
- output 3: float32 [24], P('tp')
- output 4: float32 [3072], replicated
All inputs are finite; a program needn't handle non-finite values.
Results may differ from a plain program's by a relative error of at most 0.00804819.
Values sent between devices are 32-bit elements.
A program may use at most 1 GiB of HBM per device.

v0:
```python
import jax
import jax.numpy as jnp
from jax import lax
from jax.sharding import PartitionSpec as P

HEAD_DIM = 128
ROT_DIM = 64
ROPE_BASE = 10000.0
LN_EPS = 1e-5


def layer_norm_1p(in_rows, ln_gain, ln_bias):
    rows_f32 = in_rows.astype(jnp.float32)
    row_mean = jnp.mean(rows_f32, axis=-1, keepdims=True)
    centered = rows_f32 - row_mean
    row_var = jnp.mean(centered * centered, axis=-1, keepdims=True)
    scaled = centered * lax.rsqrt(row_var + LN_EPS)
    return (scaled * (1.0 + ln_gain.astype(jnp.float32)) + ln_bias.astype(jnp.float32)).astype(jnp.bfloat16)


def rope_tables(positions):
    rot_half = ROT_DIM // 2
    inv_freq = ROPE_BASE ** (-2.0 * jnp.arange(rot_half, dtype=jnp.float32) / ROT_DIM)
    pos_angle = positions.astype(jnp.float32)[:, None] * inv_freq[None, :]
    return jnp.cos(pos_angle), jnp.sin(pos_angle)


def apply_rope(heads_in, cos_b, sin_b):
    rot_half = ROT_DIM // 2
    heads_f32 = heads_in.astype(jnp.float32)
    lead_half = heads_f32[..., :rot_half]
    tail_half = heads_f32[..., rot_half:ROT_DIM]
    turned = jnp.concatenate([lead_half * cos_b - tail_half * sin_b, tail_half * cos_b + lead_half * sin_b], axis=-1)
    return jnp.concatenate([turned.astype(jnp.bfloat16), heads_in[..., ROT_DIM:]], axis=-1)


def attention_block(h_in, positions, w_q, w_k, w_v):
    n_batch = h_in.shape[0]
    n_seq = h_in.shape[1]
    kv_heads = w_k.shape[1] // HEAD_DIM
    q_group = w_q.shape[1] // w_k.shape[1]
    cos_t, sin_t = rope_tables(positions)
    q_proj = jnp.einsum("bsd,dn->bsn", h_in, w_q, preferred_element_type=jnp.float32).astype(jnp.bfloat16)
    q_proj = q_proj.reshape(n_batch, n_seq, kv_heads, q_group, HEAD_DIM)
    k_proj = jnp.einsum("bsd,dn->bsn", h_in, w_k, preferred_element_type=jnp.float32).astype(jnp.bfloat16)
    k_proj = k_proj.reshape(n_batch, n_seq, kv_heads, HEAD_DIM)
    v_proj = jnp.einsum("bsd,dn->bsn", h_in, w_v, preferred_element_type=jnp.float32).astype(jnp.bfloat16)
    v_proj = v_proj.reshape(n_batch, n_seq, kv_heads, HEAD_DIM)
    q_proj = apply_rope(q_proj, cos_t[None, :, None, None, :], sin_t[None, :, None, None, :])
    k_proj = apply_rope(k_proj, cos_t[None, :, None, :], sin_t[None, :, None, :])
    scores = jnp.einsum("bqkgd,bskd->bkgqs", q_proj, k_proj, preferred_element_type=jnp.float32) * HEAD_DIM ** -0.5
    causal = jnp.arange(n_seq)[:, None] >= jnp.arange(n_seq)[None, :]
    scores = jnp.where(causal, scores, -1e30)
    attn_prob = jax.nn.softmax(scores, axis=-1).astype(jnp.bfloat16)
    return jnp.einsum("bkgqs,bskd->bqkgd", attn_prob, v_proj, preferred_element_type=jnp.float32).astype(jnp.bfloat16)


def solution(mesh):
    def local_layer(hidden, positions, ln1_gain, ln1_bias, w_q, w_k, w_v, w_o, ln2_gain, ln2_bias, w_up, w_down):
        n_batch = hidden.shape[0]
        n_seq = hidden.shape[1]
        h_in = layer_norm_1p(hidden, ln1_gain, ln1_bias)
        attn_out = attention_block(h_in, positions, w_q, w_k, w_v)
        head_norm = jnp.sqrt(jnp.sum(jnp.square(attn_out.astype(jnp.float32)), axis=-1)).reshape(n_batch, n_seq, -1)
        o_part = jnp.einsum("bsn,nd->bsd", attn_out.reshape(n_batch, n_seq, -1), w_o, preferred_element_type=jnp.float32)
        o_sum = lax.psum(o_part, "tp")
        x_mid = (hidden.astype(jnp.float32) + o_sum).astype(jnp.bfloat16)
        h_mid = layer_norm_1p(x_mid, ln2_gain, ln2_bias)
        mlp_act = jnp.square(jax.nn.relu(jnp.einsum("bsd,df->bsf", h_mid, w_up, preferred_element_type=jnp.float32)))
        mlp_part = jnp.einsum("bsf,fd->bsd", mlp_act.astype(jnp.bfloat16), w_down, preferred_element_type=jnp.float32)
        mlp_sum = lax.psum(mlp_part, "tp")
        out_hidden = (x_mid.astype(jnp.float32) + mlp_sum).astype(jnp.bfloat16)
        neuron_sq = jnp.sum(jnp.square(jnp.mean(mlp_act, axis=1)), axis=0)
        head_sq = jnp.sum(jnp.square(jnp.mean(head_norm, axis=1)), axis=0)
        ln1_sq = jnp.sum(jnp.square(jnp.mean(h_in, axis=1, dtype=jnp.float32)), axis=0)
        ln2_sq = jnp.sum(jnp.square(jnp.mean(h_mid, axis=1, dtype=jnp.float32)), axis=0)
        packed = jnp.concatenate([neuron_sq, head_sq, ln1_sq + ln2_sq])
        score_roots = jnp.sqrt(lax.psum(packed, "dp"))
        ff_local = neuron_sq.shape[0]
        heads_local = head_sq.shape[0]
        f_neuron = score_roots[:ff_local]
        f_head = score_roots[ff_local:ff_local + heads_local]
        f_embed = score_roots[ff_local + heads_local:]
        return out_hidden, f_neuron, f_head, f_embed

    weight_col = P(None, "tp")
    weight_row = P("tp", None)
    return jax.shard_map(
        local_layer,
        mesh=mesh,
        in_specs=(P("dp"), P(), P(), P(), weight_col, weight_col, weight_col, weight_row, P(), P(), weight_col, weight_row),
        out_specs=(P("dp"), P("tp"), P("tp"), P()),
        check_vma=False,
    )
```

profile of v0, /device:TPU:0, one launch (start us, length us, event | category | flops | bytes accessed | tf_op | source)
XLA Modules:
  0.0 475.5 jit_solution(17503589146809469336)
XLA Ops:
  7.3 0.6 iota_compare_fusion
  7.9 1.0 convert_element_type.80
  8.9 1.3 convert_reduce_fusion.1
  10.3 1.5 fusion.30
  11.8 0.6 fusion.48
  12.5 1.2 copy-done.16
  13.7 0.6 fusion.42
  14.6 0.3 copy-done.3
  14.9 5.1 %fusion.19 = bf16[2,64,1536]{2,1,0:T(8,128)(2,1)S(1)} fusion(bf16[3072,1536]{1,0:T(8,128)(2,1)} %param.16, bf16[2,64,3072]{2,1,0:T(8,128)(2,1)S(1)} %copy-done.3, f32[3072]{0:T(1024)S(1)} %convert_element_type.75, f32[3072]{0:T(1024)S(1)} %convert_add_fusion.3, f32[2,64]{1,0:T(2,128)S(1)} %add_rsqrt_fusion.1, f32[2,64]{1,0:T(2,128)S(1)} %broadcast_multiply_fusion.1), kind=kOutput, calls=%fused_computation.15 | convolution fusion | flops 1210515456 | bytes 10642432 | tf_op jit(solution)/shard_map/bsd,dn->bsn/dot_general | solution.py:43
  20.0 0.3 reshape.161
  20.4 0.2 multiply_cosine_fusion
  20.8 0.4 subtract_convert_fusion
  21.1 0.2 slice.41
  21.5 0.8 fusion.90
  22.3 2.7 multiply_reduce_fusion
  24.9 0.3 copy.50
  25.3 0.3 reshape.162
  25.6 6.2 %fusion.5 = f32[2,64,3072]{2,1,0:T(8,128)} fusion(bf16[2,64,1536]{2,1,0:T(8,128)(2,1)S(1)} %reshape.162, bf16[1536,3072]{1,0:T(8,128)(2,1)} %param.19), kind=kOutput, calls=%fused_computation.5 | convolution fusion | flops 1207959552 | bytes 11403264 | tf_op jit(solution)/shard_map/bsn,nd->bsd/dot_general | solution.py:65
  31.9 0.2 all-reduce.5.cloned.1.call-start
  32.1 0.4 copy-done.12
  32.6 27.3 %all-reduce.3.cloned.1.call-done = f32[2,64,3072]{2,1,0:T(8,128)} async-done(((f32[2,64,3072]{2,1,0:T(8,128)}), f32[2,64,3072]{2,1,0:T(8,128)}) %all-reduce.3.cloned.1.call-update) | async-done | bytes 1572880 | tf_op jit(solution)/shard_map/psum | solution.py:66
  59.8 2.3 convert_reduce_fusion
  62.2 0.4 fusion.26
  62.6 13.1 %fusion.93 = (f32[2,4608]{1,0:T(2,128)S(1)}, bf16[2,64,4608]{2,1,0:T(8,128)(2,1)S(1)}) fusion(bf16[3072,4608]{1,0:T(8,128)(2,1)} %param.22, bf16[2,64,3072]{2,1,0:T(8,128)(2,1)S(1)} %get-tuple-element.5, f32[3072]{0:T(1024)S(1)} %convert_element_type.89, f32[3072]{0:T(1024)S(1)} %convert_add_fusion.2, f32[2,64]{1,0:T(2,128)S(1)} %add_rsqrt_fusion, ...), kind=kOutput, calls=%fused_computation.94 | convolution fusion | flops 3628588032 | bytes 30340096 | tf_op jit(solution)/shard_map/bsd,df->bsf/dot_general | solution.py:69
  75.7 12.3 %fusion.1 = f32[2,64,3072]{2,1,0:T(8,128)} fusion(bf16[4608,3072]{1,0:T(8,128)(2,1)} %param.23, bf16[2,64,4608]{2,1,0:T(8,128)(2,1)S(1)} %get-tuple-element.20), kind=kOutput, calls=%fused_computation.1 | convolution fusion | flops 3623878656 | bytes 31064064 | tf_op jit(solution)/shard_map/bsf,fd->bsd/dot_general | solution.py:70
  88.0 0.7 copy-done.8
  89.0 25.9 %all-reduce.5.cloned.1.call-done = f32[2,64,3072]{2,1,0:T(8,128)} async-done(((f32[2,64,3072]{2,1,0:T(8,128)}), f32[2,64,3072]{2,1,0:T(8,128)}) %all-reduce.5.cloned.1.call-update) | async-done | bytes 1572880 | tf_op jit(solution)/shard_map/psum | solution.py:71
  114.9 3.0 convert_reduce_fusion.2
  118.0 348.8 %psum.23 = f32[7692]{0:T(1024)S(1)} all-reduce(f32[7692]{0:T(1024)S(1)} %concatenate.17), channel_id=1, replica_groups=mesh['tp'=2,'dp'=64] {'dp'}, use_global_device_ids=true, to_apply=%region_17.18 | all-reduce | flops 7692 | bytes 61536 | tf_op jit(solution)/shard_map/psum | solution.py:78
  466.8 0.5 slice.43
  467.3 0.7 slice.44
  468.0 0.6 slice.42
  (55 shorter events, 1.3 us)
Async XLA Ops:
  7.2 4.6 copy-start
  7.2 4.6 copy-start.10
  7.2 4.6 copy-start.11
  7.2 52.6 %all-reduce.3.cloned.1.call-start = ((), (), s32[]{:S(2)}) async-start(), calls=%async_computation | async-start | bytes 3145728 | tf_op jit(solution)/shard_map/psum | solution.py:66
  7.2 4.6 copy-start.2
  11.8 2.8 copy-start.14
  11.8 2.7 copy-start.6
  11.8 1.9 copy-start.16
  13.7 1.1 copy-start.3
  20.8 0.7 copy-start.5
  20.8 0.7 copy-start.9
  31.8 0.7 copy-start.12
  31.8 0.7 copy-start.13
  31.8 28.0 %copy-start.7 = (f32[3072]{0:T(1024)S(1)}, f32[3072]{0:T(1024)}, u32[]{:S(2)}) copy-start(f32[3072]{0:T(1024)} %copy-done.6) | copy-start | bytes 36868
  31.8 28.0 %copy-start.15 = (f32[2,64]{1,0:T(2,128)S(1)}, f32[2,64]{1,0:T(2,128)}, u32[]{:S(2)}) copy-start(f32[2,64]{1,0:T(2,128)} %copy-done.14) | copy-start | bytes 1540
  31.9 83.0 %all-reduce.5.cloned.1.call-start = ((), (), s32[]{:S(2)}) async-start(), calls=%async_computation.1 | async-start | bytes 3145728 | tf_op jit(solution)/shard_map/psum | solution.py:71
  62.2 13.5 %copy-start.4 = (bf16[2,64,3072]{2,1,0:T(8,128)(2,1)}, bf16[2,64,3072]{2,1,0:T(8,128)(2,1)S(1)}, u32[]{:S(2)}) copy-start(bf16[2,64,3072]{2,1,0:T(8,128)(2,1)S(1)} %get-tuple-element.5) | copy-start | bytes 2359300
  88.0 0.7 copy-start.8
  88.9 379.7 %copy-start.1 = (bf16[3072,512]{1,0:T(8,128)(2,1)S(1)}, bf16[3072,512]{1,0:T(8,128)(2,1)}, u32[]{:S(2)}) copy-start(bf16[3072,512]{1,0:T(8,128)(2,1)} %param.17) | copy-start | bytes 9437188
Sparse Core Ops, SparseCore 0:
  32.0 27.7 all-reduce.2
  88.1 26.6 all-reduce.4
where the time goes:
time: 476 us; the launch traced here: 475 us
  blocking collectives  349 us (73%)
  waiting for transfers between devices  53.2 us (11%)
  matrix products  41.5 us (9%)
  between operations  14.3 us (3%)
  other arithmetic  11.3 us (2%)
  local copies, waits for them, and re-layouts  6.13 us (1%)
    psum x1, blocking collectives, local_layer(): score_roots = jnp.sqrt(lax.psum(packed, 'dp'))  349 us
    psum x1, waiting for transfers between devices, local_layer(): o_sum = lax.psum(o_part, 'tp')  27.3 us
    psum x1, waiting for transfers between devices, local_layer(): mlp_sum = lax.psum(mlp_part, 'tp')  25.9 us
    dot_general x1, matrix products, local_layer(): jnp.einsum('bsd,df->bsf', h_mid, w_up, preferred_element_type=jnp.float32)  13.1 us
    dot_general x1, matrix products, local_layer(): jnp.einsum('bsf,fd->bsd', mlp_act.astype(jnp.bfloat16), w_down, preferred...  12.3 us
  transfers between devices with their start and end apart: 2, of which 2 were waited for; matrix products, arithmetic and copies ran while one was open for 0% of the time, Pallas kernels for 0%

commit v1 on v0

v1 whole, which is shorter than its diff:
```python
import functools

import jax
import jax.numpy as jnp
from jax import lax
from jax.experimental import pallas as pl
from jax.experimental.pallas import tpu as pltpu
from jax.sharding import PartitionSpec as P

HEAD_DIM = 128
ROT_DIM = 64
ROPE_BASE = 10000.0
LN_EPS = 1e-5
MESH = pl.DeviceIdType.MESH
F32 = jnp.float32
BF16 = jnp.bfloat16

SEQ = 64
ROWS = 128
D = 3072
QL = 1536
KL = 512
FL = 4608
CW = 512
UNIT = 1536
NU = 32
N_O = D // CW
N_UP = FL // CW
N_DN = D // CW
DN_U = FL // UNIT
EH = D + 128

O_U = 10
UP_U = 16
DN_B = 2


def rope_tables(positions):
    half = ROT_DIM // 2
    inv_freq = ROPE_BASE ** (-2.0 * jnp.arange(half, dtype=F32) / ROT_DIM)
    angle = positions.astype(F32)[:, None] * inv_freq[None, :]
    cos, sin = jnp.cos(angle), jnp.sin(angle)
    zero = jnp.zeros_like(sin)
    one = jnp.ones_like(sin)
    keep = jnp.concatenate([cos, cos, one, one], axis=1)
    from_right = jnp.concatenate([-sin, zero, zero, zero], axis=1)
    from_left = jnp.concatenate([zero, sin, zero, zero], axis=1)
    return jnp.stack([keep, from_right, from_left])


def body(sizes, x_hbm, rope_ref, ln_ref, wq, wk, wv, wo, wup, wdn,
         y_hbm, fn_ref, fh_ref, fe_ref,
         wbuf, xb, hb, xm, qs, ks, vs, at, act, osend, orecv, dsend, drecv,
         nsc, esc, are, arn,
         w_sem, d_sem, x_sem, y_sem, tp_send, tp_recv, ar_send, ar_recv):
    dims = sizes
    tp = lax.axis_index("tp")
    dp = lax.axis_index("dp")
    sz, sy, sx = dims
    axes = (
        (lax.rem(dp, sx), sx, 1),
        (lax.rem(lax.div(dp, sx), sy), sy, sx),
        (lax.div(dp, sx * sy), sz, sx * sy),
    )
    partner = 1 - tp

    def peer(axis, k):
        idx, size, stride = axes[axis]
        other = lax.rem(idx + k, size)
        return dp + (other - idx) * stride

    def slot(u, n):
        return wbuf.at[pl.ds(u * UNIT, n * UNIT), :]

    def cols(ref, c):
        return ref.at[:, pl.ds(c * CW, CW)]

    def copy_k():
        return pltpu.make_async_copy(wk, slot(6, 2), w_sem.at[0])

    def copy_v():
        return pltpu.make_async_copy(wv, slot(8, 2), w_sem.at[1])

    def copy_q(c):
        return pltpu.make_async_copy(cols(wq, c), slot(2 * c, 2), w_sem.at[2 + c])

    def copy_o(c):
        return pltpu.make_async_copy(cols(wo, c), slot(O_U + c, 1), w_sem.at[5 + c])

    def up_unit(c):
        return lax.rem(UP_U + 2 * c, NU)

    def copy_up(c):
        return pltpu.make_async_copy(cols(wup, c), slot(up_unit(c), 2), w_sem.at[11 + c])

    def copy_dn(c, u):
        return pltpu.make_async_copy(
            wdn.at[pl.ds(u * UNIT, UNIT), pl.ds(c * CW, CW)],
            slot(DN_B + DN_U * c + u, 1), d_sem.at[DN_U * c + u])

    def start_dn(c):
        for u in range(DN_U):
            copy_dn(c, u).start()

    copy_x = pltpu.make_async_copy(x_hbm, xb, x_sem)
    copy_x.start()
    copy_k().start()
    copy_v().start()
    for c in range(3):
        copy_q(c).start()
    for c in range(N_O):
        copy_o(c).start()
    for c in range(N_UP - 1):
        copy_up(c).start()

    barrier = pltpu.get_barrier_semaphore()
    pl.semaphore_signal(barrier, inc=1, device_id={"tp": partner}, device_id_type=MESH)
    n_peers = 1
    for axis in range(3):
        for k in range(1, axes[axis][1]):
            pl.semaphore_signal(barrier, inc=1, device_id={"dp": peer(axis, k)}, device_id_type=MESH)
            n_peers += 1

    def layer_norm(src, dst, which):
        gain = 1.0 + ln_ref[pl.ds(2 * which, 1), :]
        bias = ln_ref[pl.ds(2 * which + 1, 1), :]
        total = None
        for b in range(ROWS // SEQ):
            def block(i, acc):
                rows = pl.ds(pl.multiple_of(b * SEQ + i * 16, 16), 16)
                v = src[rows, :].astype(F32)
                mean = jnp.mean(v, axis=-1, keepdims=True)
                cen = v - mean
                var = jnp.mean(cen * cen, axis=-1, keepdims=True)
                h = (cen * lax.rsqrt(var + LN_EPS) * gain + bias).astype(BF16)
                dst[rows, :] = h
                return acc + jnp.sum(h.astype(F32), axis=0, keepdims=True)
            acc = lax.fori_loop(0, SEQ // 16, block, jnp.zeros((1, D), F32))
            mean_tok = acc * (1.0 / SEQ)
            sq = mean_tok * mean_tok
            total = sq if total is None else total + sq
        return total

    copy_x.wait()
    esc[:, pl.ds(0, D)] = layer_norm(xb, hb, 0)

    def proj(u):
        return jnp.dot(hb[...], wbuf[pl.ds(u * UNIT, 2 * UNIT), :], preferred_element_type=F32)

    keep = jnp.concatenate([rope_ref[0], rope_ref[0]], axis=0)
    from_right = jnp.concatenate([rope_ref[1], rope_ref[1]], axis=0)
    from_left = jnp.concatenate([rope_ref[2], rope_ref[2]], axis=0)

    def rope(v):
        u = v.astype(BF16).astype(F32)
        r = pltpu.roll(u, HEAD_DIM - ROT_DIM // 2, 1)
        l = pltpu.roll(u, ROT_DIM // 2, 1)
        return (u * keep + r * from_right + l * from_left).astype(BF16)

    copy_k().wait()
    kk = proj(6)
    for g in range(4):
        ks[pl.ds(g * ROWS, ROWS), :] = rope(kk[:, g * HEAD_DIM:(g + 1) * HEAD_DIM])
    copy_v().wait()
    vv = proj(8)
    vs[...] = vv.astype(BF16)

    row = lax.broadcasted_iota(jnp.int32, (3 * ROWS, ROWS), 0) & (ROWS - 1)
    col = lax.broadcasted_iota(jnp.int32, (3 * ROWS, ROWS), 1)
    same = (row >= SEQ) == (col >= SEQ)
    allowed = same & (col <= row)
    blocked = jnp.where(same, F32(-1e30), F32(-jnp.inf))
    lane = lax.broadcasted_iota(jnp.int32, (1, ROWS), 1)

    def attention(g, head_sq):
        q = qs[pl.ds(g * 3 * ROWS, 3 * ROWS), :]
        k = ks[pl.ds(g * ROWS, ROWS), :]
        v = vs[:, g * HEAD_DIM:(g + 1) * HEAD_DIM]
        s = lax.dot_general(q, k, (((1,), (1,)), ((), ())), preferred_element_type=F32) * HEAD_DIM ** -0.5
        s = jnp.where(allowed, s, blocked)
        e = jnp.exp(s - jnp.max(s, axis=-1, keepdims=True))
        p = (e / jnp.sum(e, axis=-1, keepdims=True)).astype(BF16)
        o = jnp.dot(p, v, preferred_element_type=F32).astype(BF16)
        of = o.astype(F32)
        norm = jnp.sqrt(jnp.sum(of * of, axis=-1, keepdims=True))
        for j in range(3):
            i = 3 * g + j
            at[:, i * HEAD_DIM:(i + 1) * HEAD_DIM] = o[j * ROWS:(j + 1) * ROWS, :]
            m0 = jnp.sum(norm[j * ROWS:j * ROWS + SEQ], axis=0, keepdims=True) * (1.0 / SEQ)
            m1 = jnp.sum(norm[j * ROWS + SEQ:(j + 1) * ROWS], axis=0, keepdims=True) * (1.0 / SEQ)
            head_sq = head_sq + jnp.where(lane == i, m0 * m0 + m1 * m1, 0.0)
        return head_sq

    head_sq = jnp.zeros((1, ROWS), F32)
    ready = ((0,), (1,), (2, 3))
    for c in range(3):
        copy_q(c).wait()
        qq = proj(2 * c)
        if c == 0:
            copy_up(N_UP - 1).start()
        for j in range(4):
            qs[pl.ds((4 * c + j) * ROWS, ROWS), :] = rope(qq[:, j * HEAD_DIM:(j + 1) * HEAD_DIM])
        if c == 2:
            start_dn(0)
            start_dn(1)
        for g in ready[c]:
            head_sq = attention(g, head_sq)
    esc[:, pl.ds(D, 128)] = head_sq

    def send_o(c):
        return pltpu.make_async_remote_copy(
            src_ref=osend.at[c], dst_ref=orecv.at[c],
            send_sem=tp_send.at[c], recv_sem=tp_recv.at[c],
            device_id={"tp": partner}, device_id_type=MESH)

    def send_d(c):
        return pltpu.make_async_remote_copy(
            src_ref=dsend.at[c], dst_ref=drecv.at[c],
            send_sem=tp_send.at[N_O + c], recv_sem=tp_recv.at[N_O + c],
            device_id={"tp": partner}, device_id_type=MESH)

    pl.semaphore_wait(barrier, n_peers)

    def finish_o(c):
        send_o(c).wait_recv()
        cs = pl.ds(c * CW, CW)
        xm[:, cs] = (xb[:, cs].astype(F32) + (osend[c] + orecv[c])).astype(BF16)

    for c in range(N_O):
        copy_o(c).wait()
        osend[c] = jnp.dot(at[...], wbuf[pl.ds((O_U + c) * UNIT, UNIT), :], preferred_element_type=F32)
        send_o(c).start()
        if c == 0:
            start_dn(2)
        if c == 3:
            start_dn(3)
        if c >= 1:
            finish_o(c - 1)
    finish_o(N_O - 1)

    esc[:, pl.ds(0, D)] = esc[:, pl.ds(0, D)] + layer_norm(xm, hb, 1)

    def ar_copy(buf, group, axis, k):
        idx = axes[axis][0]
        return pltpu.make_async_remote_copy(
            src_ref=buf.at[axis, idx], dst_ref=buf.at[axis, idx],
            send_sem=ar_send.at[group, axis, k - 1], recv_sem=ar_recv.at[group, axis, k - 1],
            device_id={"dp": peer(axis, k)}, device_id_type=MESH)

    def ar_start(buf, group, axis, value):
        buf[axis, axes[axis][0]] = value
        for k in range(1, axes[axis][1]):
            ar_copy(buf, group, axis, k).start()

    def ar_finish(buf, group, axis):
        for k in range(1, axes[axis][1]):
            ar_copy(buf, group, axis, k).wait()
        total = buf[axis, 0]
        for j in range(1, axes[axis][1]):
            total = total + buf[axis, j]
        return total

    ar_start(are, 0, 0, esc[...])

    def up_chunk(c, _):
        copy_up(c).wait()
        u = jnp.dot(hb[...], wbuf[pl.ds(pl.multiple_of(up_unit(c) * UNIT, UNIT), 2 * UNIT), :],
                    preferred_element_type=F32)
        r = jnp.maximum(u, 0.0)
        a = r * r
        cs = pl.ds(pl.multiple_of(c * CW, CW), CW)
        act[:, cs] = a.astype(BF16)
        m0 = jnp.sum(a[:SEQ], axis=0, keepdims=True) * (1.0 / SEQ)
        m1 = jnp.sum(a[SEQ:], axis=0, keepdims=True) * (1.0 / SEQ)
        nsc[:, cs] = m0 * m0 + m1 * m1
        return 0

    lax.fori_loop(0, 2, up_chunk, 0)
    start_dn(4)
    start_dn(5)
    lax.fori_loop(2, 4, up_chunk, 0)
    ar_start(are, 0, 1, ar_finish(are, 0, 0))
    lax.fori_loop(4, 7, up_chunk, 0)
    ar_start(are, 0, 2, ar_finish(are, 0, 1))
    lax.fori_loop(7, N_UP, up_chunk, 0)
    ar_start(arn, 1, 0, nsc[...])

    def out_copy(c):
        cs = pl.ds(c * CW, CW)
        return pltpu.make_async_copy(xb.at[:, cs], y_hbm.at[:, cs], y_sem.at[c])

    def finish_d(c):
        send_d(c).wait_recv()
        cs = pl.ds(c * CW, CW)
        xb[:, cs] = (xm[:, cs].astype(F32) + (dsend[c] + drecv[c])).astype(BF16)
        out_copy(c).start()

    def down_chunk(c):
        acc = None
        for u in range(DN_U):
            copy_dn(c, u).wait()
            part = jnp.dot(act[:, pl.ds(u * UNIT, UNIT)],
                           wbuf[pl.ds((DN_B + DN_U * c + u) * UNIT, UNIT), :],
                           preferred_element_type=F32)
            acc = part if acc is None else acc + part
        dsend[c] = acc
        send_d(c).start()

    def finish_e():
        total = jnp.sqrt(ar_finish(are, 0, 2))
        fe_ref[...] = total[:, :D]
        fh_ref[...] = total[:, D:]

    for c in range(N_DN):
        down_chunk(c)
        if c >= 1:
            finish_d(c - 1)
        if c == 1:
            finish_e()
            ar_start(arn, 1, 1, ar_finish(arn, 1, 0))
        if c == 4:
            ar_start(arn, 1, 2, ar_finish(arn, 1, 1))
    finish_d(N_DN - 1)
    fn_ref[...] = jnp.sqrt(ar_finish(arn, 1, 2))

    for c in range(N_O):
        send_o(c).wait_send()
    for c in range(N_DN):
        send_d(c).wait_send()
        out_copy(c).wait()


def solution(mesh):
    dims = (4, 4, 4)

    def local_layer(hidden, positions, ln1_gain, ln1_bias, w_q, w_k, w_v, w_o, ln2_gain, ln2_bias, w_up, w_down):
        ln = jnp.stack([ln1_gain, ln1_bias, ln2_gain, ln2_bias]).astype(F32)
        rope = rope_tables(positions)
        any_spec = pl.BlockSpec(memory_space=pltpu.HBM)
        vmem = pl.BlockSpec(memory_space=pltpu.VMEM)
        y, fn, fh, fe = pl.pallas_call(
            functools.partial(body, dims),
            out_shape=(
                jax.ShapeDtypeStruct((ROWS, D), BF16),
                jax.ShapeDtypeStruct((1, FL), F32),
                jax.ShapeDtypeStruct((1, 128), F32),
                jax.ShapeDtypeStruct((1, D), F32),
            ),
            in_specs=[any_spec, vmem, vmem] + [any_spec] * 6,
            out_specs=(any_spec, vmem, vmem, vmem),
            scratch_shapes=[
                pltpu.VMEM((NU * UNIT, CW), BF16),
                pltpu.VMEM((ROWS, D), BF16),
                pltpu.VMEM((ROWS, D), BF16),
                pltpu.VMEM((ROWS, D), BF16),
                pltpu.VMEM((12 * ROWS, HEAD_DIM), BF16),
                pltpu.VMEM((4 * ROWS, HEAD_DIM), BF16),
                pltpu.VMEM((ROWS, KL), BF16),
                pltpu.VMEM((ROWS, QL), BF16),
                pltpu.VMEM((ROWS, FL), BF16),
                pltpu.VMEM((N_O, ROWS, CW), F32),
                pltpu.VMEM((N_O, ROWS, CW), F32),
                pltpu.VMEM((N_DN, ROWS, CW), F32),
                pltpu.VMEM((N_DN, ROWS, CW), F32),
                pltpu.VMEM((1, FL), F32),
                pltpu.VMEM((1, EH), F32),
                pltpu.VMEM((3, 4, 1, EH), F32),
                pltpu.VMEM((3, 4, 1, FL), F32),
                pltpu.SemaphoreType.DMA((20,)),
                pltpu.SemaphoreType.DMA((N_DN * DN_U,)),
                pltpu.SemaphoreType.DMA,
                pltpu.SemaphoreType.DMA((N_DN,)),
                pltpu.SemaphoreType.DMA((N_O + N_DN,)),
                pltpu.SemaphoreType.DMA((N_O + N_DN,)),
                pltpu.SemaphoreType.DMA((2, 3, 3)),
                pltpu.SemaphoreType.DMA((2, 3, 3)),
            ],
            compiler_params=pltpu.CompilerParams(
                collective_id=0, has_side_effects=True, vmem_limit_bytes=67043328),
            name="layer",
        )(hidden.reshape(ROWS, D), rope, ln, w_q, w_k, w_v, w_o, w_up, w_down)
        return y.reshape(hidden.shape), fn.reshape(FL), fh[0, :12], fe.reshape(D)

    weight_col = P(None, "tp")
    weight_row = P("tp", None)
    return jax.shard_map(
        local_layer,
        mesh=mesh,
        in_specs=(P("dp"), P(), P(), P(), weight_col, weight_col, weight_col, weight_row, P(), P(), weight_col, weight_row),
        out_specs=(P("dp"), P("tp"), P("tp"), P()),
        check_vma=False,
    )
```

time: 476 us -> 69.3 us (0.15)
  the two profiles are of different devices: /device:TPU:0 before, /device:TPU:1 now
where the time goes in v1:
time: 69.3 us; the launch traced here: 68.9 us
  Pallas kernels  57 us (82%)
  local copies, waits for them, and re-layouts  7.52 us (11%)
  other arithmetic  3.64 us (5%)
    pallas_call x1, Pallas kernels, local_layer(): pl.pallas_call(functools.partial(body, dims), out_shape=(jax.ShapeDtypeSt...  57 us
    unnamed x2, local copies, waits for them, and re-layouts  3.37 us
    another operation x4, local copies, waits for them, and re-layouts, local_layer(): ln = jnp.stack([ln1_gain, ln1_bias, ln2_gain, ln2_bias]).astype(F32)  2.8 us

profile of v1, /device:TPU:1, one launch (start us, length us, event | category | flops | bytes accessed | tf_op | source)
XLA Modules:
  0.0 68.9 jit_solution(4392462436060120152)
XLA Ops:
  0.6 0.7 convert_element_type.6
  1.3 0.1 pad.13.clone
  1.4 0.1 pad.10.clone
  1.5 0.7 %stack.31 = bf16[1,3072]{1,0:T(2,128)(2,1)S(1)} reshape(bf16[3072]{0:T(1024)(128)(2,1)} %param.14) | data formatting | bytes 12288 | tf_op jit(solution)/shard_map/stack | solution.py:337
  2.2 0.7 %stack.32 = bf16[1,3072]{1,0:T(2,128)(2,1)S(1)} reshape(bf16[3072]{0:T(1024)(128)(2,1)} %param.15) | data formatting | bytes 12288 | tf_op jit(solution)/shard_map/stack | solution.py:337
  2.9 0.7 %stack.33 = bf16[1,3072]{1,0:T(2,128)(2,1)S(1)} reshape(bf16[3072]{0:T(1024)(128)(2,1)} %param.20) | data formatting | bytes 12288 | tf_op jit(solution)/shard_map/stack | solution.py:337
  3.6 0.7 %stack.34 = bf16[1,3072]{1,0:T(2,128)(2,1)S(1)} reshape(bf16[3072]{0:T(1024)(128)(2,1)} %param.21) | data formatting | bytes 12288 | tf_op jit(solution)/shard_map/stack | solution.py:337
  4.3 0.7 maximum_convert_fusion.ln_ref
  4.9 0.2 multiply_cosine_fusion
  5.1 0.1 maximum_bitcast_fusion
  5.3 0.7 pad_maximum_fusion.rope_ref
  5.9 57.0 %layer.1 = (bf16[128,3072]{1,0:T(8,128)(2,1)}, f32[1,4608]{1,0:T(1,128)}, f32[1,128]{1,0:T(1,128)}, f32[1,3072]{1,0:T(1,128)}) custom-call(bf16[128,3072]{1,0:T(8,128)(2,1)} %bitcast.11, f32[3,64,128]{2,1,0:T(8,128)} %pad_maximum_fusion.rope_ref, f32[4,3072]{1,0:T(4,128)} %maximum_convert_fusion.ln_ref, bf16[3072,1536]{1,0:T(8,128)(2,1)} %wq.1, ...), custom_call_target="tpu_custom_call" | custom-call | tf_op jit(solution)/shard_map/layer/pallas_call | solution.py:341
  62.9 1.2 %slice_bitcast_fusion = f32[12]{0:T(128)} fusion(f32[1,128]{1,0:T(1,128)} %get-tuple-element.10), kind=kLoop, calls=%fused_computation.8 | loop fusion | bytes 96 | tf_op jit(solution)/shard_map/squeeze | solution.py:382
  64.1 1.4 %reduce = f32[4608]{0:T(1024)} reduce(f32[1,4608]{1,0:T(1,128)} %get-tuple-element.9, f32[]{:T(128)} %constant.16), dimensions={0}, to_apply=%get-tuple-element.9.reduce_sub_computation | reduce | bytes 36868 | tf_op jit(solution)/shard_map/layer/pallas_call | solution.py:341
  65.5 2.1 %copy.18 = bf16[2,64,3072]{2,1,0:T(8,128)(2,1)} copy(bf16[2,64,3072]{2,1,0:T(8,128)(2,1)} %bitcast.12) | data formatting | bytes 1572864
  67.5 1.3 %copy.19 = f32[3072]{0:T(1024)} copy(f32[3072]{0:T(1024)} %bitcast.13) | data formatting | bytes 24576
  (6 shorter events, 0.0 us)

commit v2 on v1

--- a/solution.py
+++ b/solution.py
@@ -2,6 +2,7 @@
 
 import jax
 import jax.numpy as jnp
+import numpy as np
 from jax import lax
 from jax.experimental import pallas as pl
 from jax.experimental.pallas import tpu as pltpu
@@ -26,6 +27,7 @@
 NU = 32
 N_O = D // CW
 N_UP = FL // CW
+PN = FL // 3
 N_DN = D // CW
 DN_U = FL // UNIT
 EH = D + 128
@@ -35,24 +37,17 @@
 DN_B = 2
 
 
-def rope_tables(positions):
+def inv_freq_row():
     half = ROT_DIM // 2
-    inv_freq = ROPE_BASE ** (-2.0 * jnp.arange(half, dtype=F32) / ROT_DIM)
-    angle = positions.astype(F32)[:, None] * inv_freq[None, :]
-    cos, sin = jnp.cos(angle), jnp.sin(angle)
-    zero = jnp.zeros_like(sin)
-    one = jnp.ones_like(sin)
-    keep = jnp.concatenate([cos, cos, one, one], axis=1)
-    from_right = jnp.concatenate([-sin, zero, zero, zero], axis=1)
-    from_left = jnp.concatenate([zero, sin, zero, zero], axis=1)
-    return jnp.stack([keep, from_right, from_left])
-
-
-def body(sizes, x_hbm, rope_ref, ln_ref, wq, wk, wv, wo, wup, wdn,
-         y_hbm, fn_ref, fh_ref, fe_ref,
-         wbuf, xb, hb, xm, qs, ks, vs, at, act, osend, orecv, dsend, drecv,
+    freq = ROPE_BASE ** (-2.0 * np.arange(half, dtype=np.float64) / ROT_DIM)
+    return np.concatenate([freq, freq, np.zeros(HEAD_DIM - ROT_DIM)])[None, :].astype(np.float32)
+
+
+def body(sizes, x_hbm, pos_hbm, freq_hbm, g1, b1, g2, b2, wq, wk, wv, wo, wup, wdn,
+         y_ref, fn_ref, fh_ref, fe_ref,
+         wbuf, ln0, ln1, ln2, ln3, posb, freqb, xb, hb, xm, qs, ks, vs, at, act, osend, orecv, dsend, drecv,
          nsc, esc, are, arn,
-         w_sem, d_sem, x_sem, y_sem, tp_send, tp_recv, ar_send, ar_recv):
+         w_sem, d_sem, x_sem, tp_send, tp_recv, ar_send, ar_recv):
     dims = sizes
     tp = lax.axis_index("tp")
     dp = lax.axis_index("dp")
@@ -102,28 +97,33 @@
         for u in range(DN_U):
             copy_dn(c, u).start()
 
-    copy_x = pltpu.make_async_copy(x_hbm, xb, x_sem)
-    copy_x.start()
-    copy_k().start()
-    copy_v().start()
-    for c in range(3):
-        copy_q(c).start()
-    for c in range(N_O):
-        copy_o(c).start()
-    for c in range(N_UP - 1):
-        copy_up(c).start()
+    def copy_x():
+        return pltpu.make_async_copy(x_hbm, xb, x_sem.at[0])
+
+    lnb = (ln0, ln1, ln2, ln3)
+    small = [pltpu.make_async_copy(r, lnb[i], x_sem.at[1 + i]) for i, r in enumerate((g1, b1, g2, b2))]
+    small.append(pltpu.make_async_copy(pos_hbm, posb, x_sem.at[5]))
+    small.append(pltpu.make_async_copy(freq_hbm, freqb, x_sem.at[6]))
 
     barrier = pltpu.get_barrier_semaphore()
-    pl.semaphore_signal(barrier, inc=1, device_id={"tp": partner}, device_id_type=MESH)
-    n_peers = 1
+    greet = [{"tp": partner}]
     for axis in range(3):
         for k in range(1, axes[axis][1]):
-            pl.semaphore_signal(barrier, inc=1, device_id={"dp": peer(axis, k)}, device_id_type=MESH)
-            n_peers += 1
+            greet.append({"dp": peer(axis, k)})
+    first = [lambda: [copy_x().start()], lambda: [c.start() for c in small],
+             lambda: [copy_k().start()], lambda: [copy_v().start()]]
+    first += [lambda c=c: [copy_q(c).start()] for c in range(3)]
+    first += [lambda c=c: [copy_o(c).start()] for c in range(N_O)]
+    for i in range(max(len(first), len(greet))):
+        if i < len(first):
+            first[i]()
+        if i < len(greet):
+            pl.semaphore_signal(barrier, inc=1, device_id=greet[i], device_id_type=MESH)
+    n_peers = len(greet)
 
     def layer_norm(src, dst, which):
-        gain = 1.0 + ln_ref[pl.ds(2 * which, 1), :]
-        bias = ln_ref[pl.ds(2 * which + 1, 1), :]
+        gain = 1.0 + lnb[2 * which][...].astype(F32).reshape(1, D)
+        bias = lnb[2 * which + 1][...].astype(F32).reshape(1, D)
         total = None
         for b in range(ROWS // SEQ):
             def block(i, acc):
@@ -141,15 +141,29 @@
             total = sq if total is None else total + sq
         return total
 
-    copy_x.wait()
+    for c in small:
+        c.wait()
+    diag = (lax.broadcasted_iota(jnp.int32, (SEQ, SEQ), 0)
+            == lax.broadcasted_iota(jnp.int32, (SEQ, SEQ), 1))
+    pos_row = jnp.broadcast_to(posb[...].astype(F32).reshape(1, SEQ), (SEQ, SEQ))
+    pos_col = jnp.sum(jnp.where(diag, pos_row, 0.0), axis=1, keepdims=True)
+    angle = pos_col * freqb[...]
+    cos, sin = jnp.cos(angle), jnp.sin(angle)
+    hl = lax.broadcasted_iota(jnp.int32, (SEQ, HEAD_DIM), 1)
+    keep = jnp.where(hl < ROT_DIM, cos, 1.0)
+    from_right = jnp.where(hl < ROT_DIM // 2, -sin, 0.0)
+    from_left = jnp.where((hl >= ROT_DIM // 2) & (hl < ROT_DIM), sin, 0.0)
+    keep = jnp.concatenate([keep, keep], axis=0)
+    from_right = jnp.concatenate([from_right, from_right], axis=0)
+    from_left = jnp.concatenate([from_left, from_left], axis=0)
+
+    copy_x().wait()
+    copy_up(0).start()
+    copy_up(1).start()
     esc[:, pl.ds(0, D)] = layer_norm(xb, hb, 0)
 
     def proj(u):
         return jnp.dot(hb[...], wbuf[pl.ds(u * UNIT, 2 * UNIT), :], preferred_element_type=F32)
-
-    keep = jnp.concatenate([rope_ref[0], rope_ref[0]], axis=0)
-    from_right = jnp.concatenate([rope_ref[1], rope_ref[1]], axis=0)
-    from_left = jnp.concatenate([rope_ref[2], rope_ref[2]], axis=0)
 
     def rope(v):
         u = v.astype(BF16).astype(F32)
@@ -158,10 +172,14 @@
         return (u * keep + r * from_right + l * from_left).astype(BF16)
 
     copy_k().wait()
+    copy_up(2).start()
+    copy_up(3).start()
     kk = proj(6)
     for g in range(4):
         ks[pl.ds(g * ROWS, ROWS), :] = rope(kk[:, g * HEAD_DIM:(g + 1) * HEAD_DIM])
     copy_v().wait()
+    copy_up(4).start()
+    copy_up(5).start()
     vv = proj(8)
     vs[...] = vv.astype(BF16)
 
@@ -195,6 +213,9 @@
     ready = ((0,), (1,), (2, 3))
     for c in range(3):
         copy_q(c).wait()
+        if c == 0:
+            copy_up(6).start()
+            copy_up(7).start()
         qq = proj(2 * c)
         if c == 0:
             copy_up(N_UP - 1).start()
@@ -240,27 +261,44 @@
 
     esc[:, pl.ds(0, D)] = esc[:, pl.ds(0, D)] + layer_norm(xm, hb, 1)
 
-    def ar_copy(buf, group, axis, k):
+    def ar_copy(buf, group, phase, axis, k):
         idx = axes[axis][0]
         return pltpu.make_async_remote_copy(
-            src_ref=buf.at[axis, idx], dst_ref=buf.at[axis, idx],
-            send_sem=ar_send.at[group, axis, k - 1], recv_sem=ar_recv.at[group, axis, k - 1],
+            src_ref=buf.at[phase, idx], dst_ref=buf.at[phase, idx],
+            send_sem=ar_send.at[group, phase, k - 1], recv_sem=ar_recv.at[group, phase, k - 1],
             device_id={"dp": peer(axis, k)}, device_id_type=MESH)
 
-    def ar_start(buf, group, axis, value):
-        buf[axis, axes[axis][0]] = value
+    def ar_start(buf, group, phase, axis, value):
+        buf[phase, axes[axis][0]] = value
         for k in range(1, axes[axis][1]):
-            ar_copy(buf, group, axis, k).start()
-
-    def ar_finish(buf, group, axis):
+            ar_copy(buf, group, phase, axis, k).start()
+
+    def ar_finish(buf, group, phase, axis):
         for k in range(1, axes[axis][1]):
-            ar_copy(buf, group, axis, k).wait()
-        total = buf[axis, 0]
+            ar_copy(buf, group, phase, axis, k).wait()
+        total = buf[phase, 0]
         for j in range(1, axes[axis][1]):
-            total = total + buf[axis, j]
+            total = total + buf[phase, j]
         return total
 
-    ar_start(are, 0, 0, esc[...])
+    def e_start(phase, value):
+        ar_start(are, 3, phase, phase, value)
+
+    def e_finish(phase):
+        return ar_finish(are, 3, phase, phase)
+
+    def n_step(phase):
+        for part in range(3):
+            if phase == 0:
+                value = nsc[:, pl.ds(part * PN, PN)]
+            else:
+                value = ar_finish(arn.at[part], part, phase - 1, (part + phase - 1) % 3)
+            if phase < 3:
+                ar_start(arn.at[part], part, phase, (part + phase) % 3, value)
+            else:
+                fn_ref[pl.ds(part * PN, PN)] = jnp.sqrt(value).reshape(PN)
+
+    e_start(0, esc[...])
 
     def up_chunk(c, _):
         copy_up(c).wait()
@@ -277,25 +315,33 @@
 
     lax.fori_loop(0, 2, up_chunk, 0)
     start_dn(4)
-    start_dn(5)
     lax.fori_loop(2, 4, up_chunk, 0)
-    ar_start(are, 0, 1, ar_finish(are, 0, 0))
-    lax.fori_loop(4, 7, up_chunk, 0)
-    ar_start(are, 0, 2, ar_finish(are, 0, 1))
-    lax.fori_loop(7, N_UP, up_chunk, 0)
-    ar_start(arn, 1, 0, nsc[...])
-
-    def out_copy(c):
-        cs = pl.ds(c * CW, CW)
-        return pltpu.make_async_copy(xb.at[:, cs], y_hbm.at[:, cs], y_sem.at[c])
+    copy_dn(5, 0).start()
+    lax.fori_loop(4, 6, up_chunk, 0)
+    copy_dn(5, 1).start()
+    lax.fori_loop(6, N_UP, up_chunk, 0)
+    n_step(0)
+    copy_dn(5, 2).start()
+    e_start(1, e_finish(0))
 
     def finish_d(c):
         send_d(c).wait_recv()
         cs = pl.ds(c * CW, CW)
-        xb[:, cs] = (xm[:, cs].astype(F32) + (dsend[c] + drecv[c])).astype(BF16)
-        out_copy(c).start()
-
-    def down_chunk(c):
+        y_ref[:, cs] = (xm[:, cs].astype(F32) + (dsend[c] + drecv[c])).astype(BF16)
+
+    def finish_e():
+        total = jnp.sqrt(e_finish(2))
+        fe_ref[...] = total[:, :D].reshape(D)
+        fh_ref[...] = total[:, D:].reshape(128)[:12]
+
+    hooks = {
+        (1, 2): lambda: e_start(2, e_finish(1)),
+        (2, 1): lambda: n_step(1),
+        (3, 2): finish_e,
+        (4, 2): lambda: n_step(2),
+    }
+
+    for c in range(N_DN):
         acc = None
         for u in range(DN_U):
             copy_dn(c, u).wait()
@@ -303,53 +349,46 @@
                            wbuf[pl.ds((DN_B + DN_U * c + u) * UNIT, UNIT), :],
                            preferred_element_type=F32)
             acc = part if acc is None else acc + part
-        dsend[c] = acc
-        send_d(c).start()
-
-    def finish_e():
-        total = jnp.sqrt(ar_finish(are, 0, 2))
-        fe_ref[...] = total[:, :D]
-        fh_ref[...] = total[:, D:]
-
-    for c in range(N_DN):
-        down_chunk(c)
+            if u == DN_U - 1:
+                dsend[c] = acc
+                send_d(c).start()
+            if (c, u) in hooks:
+                hooks[c, u]()
         if c >= 1:
             finish_d(c - 1)
-        if c == 1:
-            finish_e()
-            ar_start(arn, 1, 1, ar_finish(arn, 1, 0))
-        if c == 4:
-            ar_start(arn, 1, 2, ar_finish(arn, 1, 1))
     finish_d(N_DN - 1)
-    fn_ref[...] = jnp.sqrt(ar_finish(arn, 1, 2))
+    n_step(3)
 
     for c in range(N_O):
         send_o(c).wait_send()
     for c in range(N_DN):
         send_d(c).wait_send()
-        out_copy(c).wait()
 
 
 def solution(mesh):
     dims = (4, 4, 4)
 
     def local_layer(hidden, positions, ln1_gain, ln1_bias, w_q, w_k, w_v, w_o, ln2_gain, ln2_bias, w_up, w_down):
-        ln = jnp.stack([ln1_gain, ln1_bias, ln2_gain, ln2_bias]).astype(F32)
-        rope = rope_tables(positions)
-        any_spec = pl.BlockSpec(memory_space=pltpu.HBM)
+        hbm = pl.BlockSpec(memory_space=pltpu.HBM)
         vmem = pl.BlockSpec(memory_space=pltpu.VMEM)
         y, fn, fh, fe = pl.pallas_call(
             functools.partial(body, dims),
             out_shape=(
-                jax.ShapeDtypeStruct((ROWS, D), BF16),
-                jax.ShapeDtypeStruct((1, FL), F32),
-                jax.ShapeDtypeStruct((1, 128), F32),
-                jax.ShapeDtypeStruct((1, D), F32),
+                pltpu.VMEM((ROWS, D), BF16),
+                pltpu.VMEM((FL,), F32),
+                pltpu.VMEM((12,), F32),
+                pltpu.VMEM((D,), F32),
             ),
-            in_specs=[any_spec, vmem, vmem] + [any_spec] * 6,
-            out_specs=(any_spec, vmem, vmem, vmem),
+            in_specs=[hbm] * 13,
+            out_specs=(vmem, vmem, vmem, vmem),
             scratch_shapes=[
                 pltpu.VMEM((NU * UNIT, CW), BF16),
+                pltpu.VMEM((D,), BF16),
+                pltpu.VMEM((D,), BF16),
+                pltpu.VMEM((D,), BF16),
+                pltpu.VMEM((D,), BF16),
+                pltpu.VMEM((SEQ,), jnp.int32),
+                pltpu.VMEM((1, HEAD_DIM), F32),
                 pltpu.VMEM((ROWS, D), BF16),
                 pltpu.VMEM((ROWS, D), BF16),
                 pltpu.VMEM((ROWS, D), BF16),
@@ -365,21 +404,21 @@
                 pltpu.VMEM((1, FL), F32),
                 pltpu.VMEM((1, EH), F32),
                 pltpu.VMEM((3, 4, 1, EH), F32),
-                pltpu.VMEM((3, 4, 1, FL), F32),
+                pltpu.VMEM((3, 3, 4, 1, PN), F32),
                 pltpu.SemaphoreType.DMA((20,)),
                 pltpu.SemaphoreType.DMA((N_DN * DN_U,)),
-                pltpu.SemaphoreType.DMA,
-                pltpu.SemaphoreType.DMA((N_DN,)),
+                pltpu.SemaphoreType.DMA((7,)),
                 pltpu.SemaphoreType.DMA((N_O + N_DN,)),
                 pltpu.SemaphoreType.DMA((N_O + N_DN,)),
-                pltpu.SemaphoreType.DMA((2, 3, 3)),
-                pltpu.SemaphoreType.DMA((2, 3, 3)),
+                pltpu.SemaphoreType.DMA((4, 3, 3)),
+                pltpu.SemaphoreType.DMA((4, 3, 3)),
             ],
             compiler_params=pltpu.CompilerParams(
-                collective_id=0, has_side_effects=True, vmem_limit_bytes=67043328),
+                collective_id=0, has_side_effects=True, vmem_limit_bytes=62 * 2**20),
             name="layer",
-        )(hidden.reshape(ROWS, D), rope, ln, w_q, w_k, w_v, w_o, w_up, w_down)
-        return y.reshape(hidden.shape), fn.reshape(FL), fh[0, :12], fe.reshape(D)
+        )(hidden.reshape(ROWS, D), positions, jnp.asarray(inv_freq_row()), ln1_gain, ln1_bias, ln2_gain, ln2_bias,
+          w_q, w_k, w_v, w_o, w_up, w_down)
+        return y.reshape(hidden.shape), fn, fh, fe
 
     weight_col = P(None, "tp")
     weight_row = P("tp", None)

time: 69.3 us -> 43.8 us (0.63)
  Pallas kernels: 57 us -> 39.8 us
  local copies, waits for them, and re-layouts: 7.52 us -> 2.6 us
  other arithmetic: 3.64 us -> 0 us
    pallas_call x1, Pallas kernels: 57 us -> 39.8 us  [local_layer(): pl.pallas_call(functools.partial(body, dims), out_shape=(pltpu.VMEM((ROWS...]
    another operation x5 -> x0, local copies, waits for them, and re-layouts: 2.81 us -> none  [the longest x4 2.8 us: local_layer(): ln = jnp.stack([ln1_gain, ln1_bias, ln2_gain, ln2_bias]).astype(F32)]
    pallas_call x1 -> x0, other arithmetic: 1.37 us -> none  [local_layer(): pl.pallas_call(functools.partial(body, dims), out_shape=(jax.ShapeDtypeSt...]
    convert_element_type x2 -> x0, other arithmetic: 1.33 us -> none  [the longest x1 0.67 us: local_layer(): ln = jnp.stack([ln1_gain, ln1_bias, ln2_gain, ln2_bias]).astype(F32)]
    squeeze x1 -> x0, local copies, waits for them, and re-layouts: 1.17 us -> none  [local_layer(): return (y.reshape(hidden.shape), fn.reshape(FL), fh[0, :12], fe.reshape(D))]
    unnamed x2 -> x4, local copies, waits for them, and re-layouts: 3.37 us -> 2.6 us
    another operation x2 -> x0, other arithmetic: 0.74 us -> none  [rope_tables(): return jnp.stack([keep, from_right, from_left])]
where the time goes in v2:
time: 43.8 us; the launch traced here: 43.1 us
  Pallas kernels  39.8 us (91%)
  local copies, waits for them, and re-layouts  2.6 us (6%)
  between operations  0.65 us (1%)
    pallas_call x1, Pallas kernels, local_layer(): pl.pallas_call(functools.partial(body, dims), out_shape=(pltpu.VMEM((ROWS...  39.8 us
    unnamed x4, local copies, waits for them, and re-layouts  2.6 us

profile of v2, /device:TPU:1, one launch (start us, length us, event | category | flops | bytes accessed | tf_op | source)
XLA Modules:
  0.0 43.1 jit_solution(3010219330803627768)
XLA Ops:
  0.6 39.8 %layer.1 = (bf16[128,3072]{1,0:T(8,128)(2,1)S(1)}, f32[4608]{0:T(1024)S(1)}, f32[12]{0:T(128)S(1)}, f32[3072]{0:T(1024)S(1)}) custom-call(bf16[128,3072]{1,0:T(8,128)(2,1)} %bitcast.3, s32[64]{0:T(128)} %pos_hbm.1, f32[1,128]{1,0:T(1,128)} %constant.2.clone.freq_hbm, bf16[3072]{0:T(1024)(128)(2,1)} %g1.1, bf16[3072]{0:T(1024)(128)(2,1)} %b1.1, ...), custom_call_target="tpu_custom_call" | custom-call | tf_op jit(solution)/shard_map/layer/pallas_call | solution.py:374
  40.5 0.9 %copy.21 = bf16[2,64,3072]{2,1,0:T(8,128)(2,1)} copy(bf16[2,64,3072]{2,1,0:T(8,128)(2,1)S(1)} %bitcast.2) | data formatting | bytes 1572864
  41.3 0.5 %copy.23 = f32[12]{0:T(128)} copy(f32[12]{0:T(128)S(1)} %get-tuple-element.14) | data formatting | bytes 96
  41.8 0.6 %copy.24 = f32[3072]{0:T(1024)} copy(f32[3072]{0:T(1024)S(1)} %get-tuple-element.15) | data formatting | bytes 24576
  42.4 0.6 %copy.22 = f32[4608]{0:T(1024)} copy(f32[4608]{0:T(1024)S(1)} %get-tuple-element.13) | data formatting | bytes 36864

commit v3 on v2

--- a/solution.py
+++ b/solution.py
@@ -88,14 +88,10 @@
     def copy_up(c):
         return pltpu.make_async_copy(cols(wup, c), slot(up_unit(c), 2), w_sem.at[11 + c])
 
-    def copy_dn(c, u):
+    def copy_dn(c, u=0, n=DN_U):
         return pltpu.make_async_copy(
-            wdn.at[pl.ds(u * UNIT, UNIT), pl.ds(c * CW, CW)],
-            slot(DN_B + DN_U * c + u, 1), d_sem.at[DN_U * c + u])
-
-    def start_dn(c):
-        for u in range(DN_U):
-            copy_dn(c, u).start()
+            wdn.at[pl.ds(u * UNIT, n * UNIT), pl.ds(c * CW, CW)],
+            slot(DN_B + DN_U * c + u, n), d_sem.at[c + u])
 
     def copy_x():
         return pltpu.make_async_copy(x_hbm, xb, x_sem.at[0])
@@ -126,23 +122,30 @@
         bias = lnb[2 * which + 1][...].astype(F32).reshape(1, D)
         total = None
         for b in range(ROWS // SEQ):
-            def block(i, acc):
-                rows = pl.ds(pl.multiple_of(b * SEQ + i * 16, 16), 16)
+            acc = None
+            for i in range(SEQ // 16):
+                rows = pl.ds(b * SEQ + i * 16, 16)
                 v = src[rows, :].astype(F32)
                 mean = jnp.mean(v, axis=-1, keepdims=True)
                 cen = v - mean
                 var = jnp.mean(cen * cen, axis=-1, keepdims=True)
                 h = (cen * lax.rsqrt(var + LN_EPS) * gain + bias).astype(BF16)
                 dst[rows, :] = h
-                return acc + jnp.sum(h.astype(F32), axis=0, keepdims=True)
-            acc = lax.fori_loop(0, SEQ // 16, block, jnp.zeros((1, D), F32))
-            mean_tok = acc * (1.0 / SEQ)
+                hf = h.astype(F32)
+                part = hf[:8] + hf[8:]
+                acc = part if acc is None else acc + part
+            mean_tok = jnp.sum(acc, axis=0, keepdims=True) * (1.0 / SEQ)
             sq = mean_tok * mean_tok
             total = sq if total is None else total + sq
         return total
 
     for c in small:
         c.wait()
+    copy_x().wait()
+    copy_up(0).start()
+    copy_up(1).start()
+    esc[:, pl.ds(0, D)] = layer_norm(xb, hb, 0)
+
     diag = (lax.broadcasted_iota(jnp.int32, (SEQ, SEQ), 0)
             == lax.broadcasted_iota(jnp.int32, (SEQ, SEQ), 1))
     pos_row = jnp.broadcast_to(posb[...].astype(F32).reshape(1, SEQ), (SEQ, SEQ))
@@ -157,11 +160,6 @@
     from_right = jnp.concatenate([from_right, from_right], axis=0)
     from_left = jnp.concatenate([from_left, from_left], axis=0)
 
-    copy_x().wait()
-    copy_up(0).start()
-    copy_up(1).start()
-    esc[:, pl.ds(0, D)] = layer_norm(xb, hb, 0)
-
     def proj(u):
         return jnp.dot(hb[...], wbuf[pl.ds(u * UNIT, 2 * UNIT), :], preferred_element_type=F32)
 
@@ -174,13 +172,13 @@
     copy_k().wait()
     copy_up(2).start()
     copy_up(3).start()
-    kk = proj(6)
-    for g in range(4):
-        ks[pl.ds(g * ROWS, ROWS), :] = rope(kk[:, g * HEAD_DIM:(g + 1) * HEAD_DIM])
     copy_v().wait()
     copy_up(4).start()
     copy_up(5).start()
+    kk = proj(6)
     vv = proj(8)
+    for g in range(4):
+        ks[pl.ds(g * ROWS, ROWS), :] = rope(kk[:, g * HEAD_DIM:(g + 1) * HEAD_DIM])
     vs[...] = vv.astype(BF16)
 
     row = lax.broadcasted_iota(jnp.int32, (3 * ROWS, ROWS), 0) & (ROWS - 1)
@@ -209,23 +207,25 @@
             head_sq = head_sq + jnp.where(lane == i, m0 * m0 + m1 * m1, 0.0)
         return head_sq
 
-    head_sq = jnp.zeros((1, ROWS), F32)
-    ready = ((0,), (1,), (2, 3))
-    for c in range(3):
-        copy_q(c).wait()
-        if c == 0:
-            copy_up(6).start()
-            copy_up(7).start()
+    def query(c):
         qq = proj(2 * c)
-        if c == 0:
-            copy_up(N_UP - 1).start()
         for j in range(4):
             qs[pl.ds((4 * c + j) * ROWS, ROWS), :] = rope(qq[:, j * HEAD_DIM:(j + 1) * HEAD_DIM])
-        if c == 2:
-            start_dn(0)
-            start_dn(1)
-        for g in ready[c]:
-            head_sq = attention(g, head_sq)
+
+    head_sq = jnp.zeros((1, ROWS), F32)
+    copy_q(0).wait()
+    copy_up(6).start()
+    copy_up(7).start()
+    copy_q(1).wait()
+    query(0)
+    query(1)
+    head_sq = attention(0, head_sq)
+    head_sq = attention(1, head_sq)
+    copy_q(2).wait()
+    copy_up(N_UP - 1).start()
+    query(2)
+    head_sq = attention(2, head_sq)
+    head_sq = attention(3, head_sq)
     esc[:, pl.ds(D, 128)] = head_sq
 
     def send_o(c):
@@ -247,17 +247,21 @@
         cs = pl.ds(c * CW, CW)
         xm[:, cs] = (xb[:, cs].astype(F32) + (osend[c] + orecv[c])).astype(BF16)
 
+    for part in range(2):
+        for c in range(3 * part, 3 * part + 3):
+            copy_o(c).wait()
+        if part == 0:
+            copy_dn(0).start()
+            copy_dn(1).start()
+        else:
+            copy_dn(2).start()
+        for c in range(3 * part, 3 * part + 3):
+            osend[c] = jnp.dot(at[...], wbuf[pl.ds((O_U + c) * UNIT, UNIT), :], preferred_element_type=F32)
+            send_o(c).start()
+        if part == 1:
+            copy_dn(3).start()
     for c in range(N_O):
-        copy_o(c).wait()
-        osend[c] = jnp.dot(at[...], wbuf[pl.ds((O_U + c) * UNIT, UNIT), :], preferred_element_type=F32)
-        send_o(c).start()
-        if c == 0:
-            start_dn(2)
-        if c == 3:
-            start_dn(3)
-        if c >= 1:
-            finish_o(c - 1)
-    finish_o(N_O - 1)
+        finish_o(c)
 
     esc[:, pl.ds(0, D)] = esc[:, pl.ds(0, D)] + layer_norm(xm, hb, 1)
 
@@ -300,28 +304,27 @@
 
     e_start(0, esc[...])
 
-    def up_chunk(c, _):
-        copy_up(c).wait()
-        u = jnp.dot(hb[...], wbuf[pl.ds(pl.multiple_of(up_unit(c) * UNIT, UNIT), 2 * UNIT), :],
-                    preferred_element_type=F32)
+    def up_chunk(c):
+        u = jnp.dot(hb[...], wbuf[pl.ds((UP_U + 2 * c) % NU * UNIT, 2 * UNIT), :], preferred_element_type=F32)
         r = jnp.maximum(u, 0.0)
         a = r * r
-        cs = pl.ds(pl.multiple_of(c * CW, CW), CW)
+        cs = pl.ds(c * CW, CW)
         act[:, cs] = a.astype(BF16)
         m0 = jnp.sum(a[:SEQ], axis=0, keepdims=True) * (1.0 / SEQ)
         m1 = jnp.sum(a[SEQ:], axis=0, keepdims=True) * (1.0 / SEQ)
         nsc[:, cs] = m0 * m0 + m1 * m1
-        return 0
-
-    lax.fori_loop(0, 2, up_chunk, 0)
-    start_dn(4)
-    lax.fori_loop(2, 4, up_chunk, 0)
-    copy_dn(5, 0).start()
-    lax.fori_loop(4, 6, up_chunk, 0)
-    copy_dn(5, 1).start()
-    lax.fori_loop(6, N_UP, up_chunk, 0)
+
+    for i, chunks in enumerate(((0, 1, 2), (3, 4, 5), (6, 7), (8,))):
+        for c in chunks:
+            copy_up(c).wait()
+        if i == 1:
+            copy_dn(4).start()
+            copy_dn(5, 0, 1).start()
+        elif i >= 2:
+            copy_dn(5, i - 1, 1).start()
+        for c in chunks:
+            up_chunk(c)
     n_step(0)
-    copy_dn(5, 2).start()
     e_start(1, e_finish(0))
 
     def finish_d(c):
@@ -335,27 +338,28 @@
         fh_ref[...] = total[:, D:].reshape(128)[:12]
 
     hooks = {
-        (1, 2): lambda: e_start(2, e_finish(1)),
-        (2, 1): lambda: n_step(1),
-        (3, 2): finish_e,
-        (4, 2): lambda: n_step(2),
+        1: lambda: n_step(1),
+        2: lambda: e_start(2, e_finish(1)),
+        3: lambda: n_step(2),
+        4: finish_e,
     }
 
     for c in range(N_DN):
         acc = None
-        for u in range(DN_U):
-            copy_dn(c, u).wait()
-            part = jnp.dot(act[:, pl.ds(u * UNIT, UNIT)],
-                           wbuf[pl.ds((DN_B + DN_U * c + u) * UNIT, UNIT), :],
+        n = DN_U if c < N_DN - 1 else 1
+        for u in range(0, DN_U, n):
+            copy_dn(c, u, n).wait()
+            part = jnp.dot(act[:, pl.ds(u * UNIT, n * UNIT)],
+                           wbuf[pl.ds((DN_B + DN_U * c + u) * UNIT, n * UNIT), :],
                            preferred_element_type=F32)
             acc = part if acc is None else acc + part
-            if u == DN_U - 1:
-                dsend[c] = acc
-                send_d(c).start()
-            if (c, u) in hooks:
-                hooks[c, u]()
-        if c >= 1:
-            finish_d(c - 1)
+        dsend[c] = acc
+        send_d(c).start()
+        if c >= 2:
+            finish_d(c - 2)
+        if c in hooks:
+            hooks[c]()
+    finish_d(N_DN - 2)
     finish_d(N_DN - 1)
     n_step(3)
 
@@ -363,6 +367,15 @@
         send_o(c).wait_send()
     for c in range(N_DN):
         send_d(c).wait_send()
+
+
+def writer(y, fn, fh, fe, y_out, fn_out, fh_out, fe_out, sem):
+    copies = [pltpu.make_async_copy(a, b, sem.at[i])
+              for i, (a, b) in enumerate(((y, y_out), (fn, fn_out), (fh, fh_out), (fe, fe_out)))]
+    for c in copies:
+        c.start()
+    for c in copies:
+        c.wait()
 
 
 def solution(mesh):
@@ -406,7 +419,7 @@
                 pltpu.VMEM((3, 4, 1, EH), F32),
                 pltpu.VMEM((3, 3, 4, 1, PN), F32),
                 pltpu.SemaphoreType.DMA((20,)),
-                pltpu.SemaphoreType.DMA((N_DN * DN_U,)),
+                pltpu.SemaphoreType.DMA((N_DN + DN_U - 1,)),
                 pltpu.SemaphoreType.DMA((7,)),
                 pltpu.SemaphoreType.DMA((N_O + N_DN,)),
                 pltpu.SemaphoreType.DMA((N_O + N_DN,)),
@@ -418,6 +431,15 @@
             name="layer",
         )(hidden.reshape(ROWS, D), positions, jnp.asarray(inv_freq_row()), ln1_gain, ln1_bias, ln2_gain, ln2_bias,
           w_q, w_k, w_v, w_o, w_up, w_down)
+        held = [pltpu.with_memory_space_constraint(v, pltpu.VMEM) for v in (y, fn, fh, fe)]
+        y, fn, fh, fe = pl.pallas_call(
+            writer,
+            out_shape=tuple(jax.ShapeDtypeStruct(v.shape, v.dtype) for v in held),
+            in_specs=[vmem] * 4,
+            out_specs=(hbm,) * 4,
+            scratch_shapes=[pltpu.SemaphoreType.DMA((4,))],
+            name="writer",
+        )(*held)
         return y.reshape(hidden.shape), fn, fh, fe
 
     weight_col = P(None, "tp")

time: 43.8 us -> 36.3 us (0.83); the launches traced: 43.1 us -> 36.1 us
  Pallas kernels: 39.8 us -> 35.3 us
  local copies, waits for them, and re-layouts: 2.6 us -> 0 us
    pallas_call x1, Pallas kernels: 39.8 us -> 34.4 us  [local_layer(): pl.pallas_call(functools.partial(body, dims), out_shape=(pltpu.VMEM((ROWS...]
    unnamed x4 -> x0, local copies, waits for them, and re-layouts: 2.6 us -> none
    pallas_call x0 -> x1, Pallas kernels: none -> 0.92 us  [local_layer(): pl.pallas_call(writer, out_shape=tuple((jax.ShapeDtypeStruct(v.shape, v.d...]
where the time goes in v3:
time: 36.3 us; the launch traced here: 36.1 us
  Pallas kernels  35.3 us (97%)
  between operations  0.8 us (2%)
    pallas_call x1, Pallas kernels, local_layer(): pl.pallas_call(functools.partial(body, dims), out_shape=(pltpu.VMEM((ROWS...  34.4 us
    pallas_call x1, Pallas kernels, local_layer(): pl.pallas_call(writer, out_shape=tuple((jax.ShapeDtypeStruct(v.shape, v.d...  0.92 us

profile of v3, /device:TPU:1, one launch (start us, length us, event | category | flops | bytes accessed | tf_op | source)
XLA Modules:
  0.0 36.1 jit_solution(3407182220162533728)
XLA Ops:
  0.6 34.4 %layer.1 = (bf16[128,3072]{1,0:T(8,128)(2,1)S(1)}, f32[4608]{0:T(1024)S(1)}, f32[12]{0:T(128)S(1)}, f32[3072]{0:T(1024)S(1)}) custom-call(bf16[128,3072]{1,0:T(8,128)(2,1)} %bitcast.2, s32[64]{0:T(128)} %pos_hbm.1, f32[1,128]{1,0:T(1,128)} %constant.2.clone.freq_hbm, bf16[3072]{0:T(1024)(128)(2,1)} %g1.1, bf16[3072]{0:T(1024)(128)(2,1)} %b1.1, ...), custom_call_target="tpu_custom_call" | custom-call | tf_op jit(solution)/shard_map/layer/pallas_call | solution.py:387
  35.1 0.9 %writer.1 = (bf16[128,3072]{1,0:T(8,128)(2,1)}, f32[4608]{0:T(1024)}, f32[12]{0:T(128)}, f32[3072]{0:T(1024)}) custom-call(bf16[128,3072]{1,0:T(8,128)(2,1)S(1)} %get-tuple-element.12.y, f32[4608]{0:T(1024)S(1)} %get-tuple-element.13.fn, f32[12]{0:T(128)S(1)} %get-tuple-element.14.fh, f32[3072]{0:T(1024)S(1)} %get-tuple-element.15.fe), custom_call_target="tpu_custom_call" | custom-call | tf_op jit(solution)/shard_map/writer/pallas_call | solution.py:435

commit v4 on v3

--- a/solution.py
+++ b/solution.py
@@ -27,7 +27,7 @@
 NU = 32
 N_O = D // CW
 N_UP = FL // CW
-PN = FL // 3
+NA = 6 * CW
 N_DN = D // CW
 DN_U = FL // UNIT
 EH = D + 128
@@ -35,6 +35,9 @@
 O_U = 10
 UP_U = 16
 DN_B = 2
+TP_SEM = (0, 0, 0, 1, 1, 1, 2, 2, 3, 3, 4, 5)
+UP_SEM = (0, 0, 0, 1, 1, 2, 3, 4)
+DN_SEM = (7, 8, 9, 10, 11, 0, 1, 2)
 
 
 def inv_freq_row():
@@ -45,24 +48,30 @@
 
 def body(sizes, x_hbm, pos_hbm, freq_hbm, g1, b1, g2, b2, wq, wk, wv, wo, wup, wdn,
          y_ref, fn_ref, fh_ref, fe_ref,
-         wbuf, ln0, ln1, ln2, ln3, posb, freqb, xb, hb, xm, qs, ks, vs, at, act, osend, orecv, dsend, drecv,
-         nsc, esc, are, arn,
-         w_sem, d_sem, x_sem, tp_send, tp_recv, ar_send, ar_recv):
+         wbuf, ln0, ln1, ln2, ln3, posb, freqb, xb, hb, xm, qs, ks, vs, at, act, xsend, xrecv,
+         nsc, esc, are, arn, arm,
+         sem, tp_send, tp_recv, ar_send, ar_recv):
     dims = sizes
     tp = lax.axis_index("tp")
     dp = lax.axis_index("dp")
     sz, sy, sx = dims
-    axes = (
-        (lax.rem(dp, sx), sx, 1),
-        (lax.rem(lax.div(dp, sx), sy), sy, sx),
-        (lax.div(dp, sx * sy), sz, sx * sy),
-    )
+    ix = lax.rem(dp, sx)
+    iy = lax.rem(lax.div(dp, sx), sy)
+    iz = lax.div(dp, sx * sy)
     partner = 1 - tp
 
-    def peer(axis, k):
-        idx, size, stride = axes[axis]
-        other = lax.rem(idx + k, size)
-        return dp + (other - idx) * stride
+    def peer(phase, k):
+        step, flip = k // 2, k % 2
+        if phase == 0:
+            to_x, to_z = lax.rem(ix + step, sx), iz
+            to_y = iy + 1 - 2 * lax.rem(iy, 2) if flip else iy
+        else:
+            to_x, to_z = ix, lax.rem(iz + step, sz)
+            to_y = sy - 1 - iy if flip else iy
+        return to_x + sx * (to_y + sy * to_z)
+
+    place = (2 * ix + lax.rem(iy, 2), 2 * iz + lax.div(iy, 2))
+    group_size = (2 * sx, 2 * sz)
 
     def slot(u, n):
         return wbuf.at[pl.ds(u * UNIT, n * UNIT), :]
@@ -70,42 +79,47 @@
     def cols(ref, c):
         return ref.at[:, pl.ds(c * CW, CW)]
 
+    def arrive(u, n, s):
+        pltpu.make_async_copy(slot(u, n), slot(u, n), sem.at[s]).wait()
+
     def copy_k():
-        return pltpu.make_async_copy(wk, slot(6, 2), w_sem.at[0])
+        return pltpu.make_async_copy(wk, slot(6, 2), sem.at[7])
 
     def copy_v():
-        return pltpu.make_async_copy(wv, slot(8, 2), w_sem.at[1])
+        return pltpu.make_async_copy(wv, slot(8, 2), sem.at[7])
 
     def copy_q(c):
-        return pltpu.make_async_copy(cols(wq, c), slot(2 * c, 2), w_sem.at[2 + c])
+        return pltpu.make_async_copy(cols(wq, c), slot(2 * c, 2), sem.at[8 + c // 2])
 
     def copy_o(c):
-        return pltpu.make_async_copy(cols(wo, c), slot(O_U + c, 1), w_sem.at[5 + c])
-
-    def up_unit(c):
-        return lax.rem(UP_U + 2 * c, NU)
+        return pltpu.make_async_copy(cols(wo, c), slot(O_U + c, 1), sem.at[10 + c // 3])
 
     def copy_up(c):
-        return pltpu.make_async_copy(cols(wup, c), slot(up_unit(c), 2), w_sem.at[11 + c])
+        return pltpu.make_async_copy(cols(wup, c), slot(UP_U + 2 * c, 2), sem.at[UP_SEM[c]])
+
+    def copy_up_half(half):
+        c = N_UP - 1
+        return pltpu.make_async_copy(wup.at[pl.ds(half * UNIT, UNIT), pl.ds(c * CW, CW)],
+                                     slot((UP_U + 2 * c) % NU + half, 1), sem.at[5 + half])
 
     def copy_dn(c, u=0, n=DN_U):
         return pltpu.make_async_copy(
             wdn.at[pl.ds(u * UNIT, n * UNIT), pl.ds(c * CW, CW)],
-            slot(DN_B + DN_U * c + u, n), d_sem.at[c + u])
+            slot(DN_B + DN_U * c + u, n), sem.at[DN_SEM[c + u]])
 
     def copy_x():
-        return pltpu.make_async_copy(x_hbm, xb, x_sem.at[0])
+        return pltpu.make_async_copy(x_hbm, xb, sem.at[0])
 
     lnb = (ln0, ln1, ln2, ln3)
-    small = [pltpu.make_async_copy(r, lnb[i], x_sem.at[1 + i]) for i, r in enumerate((g1, b1, g2, b2))]
-    small.append(pltpu.make_async_copy(pos_hbm, posb, x_sem.at[5]))
-    small.append(pltpu.make_async_copy(freq_hbm, freqb, x_sem.at[6]))
+    small = [pltpu.make_async_copy(r, lnb[i], sem.at[1 + i]) for i, r in enumerate((g1, b1, g2, b2))]
+    small.append(pltpu.make_async_copy(pos_hbm, posb, sem.at[5]))
+    small.append(pltpu.make_async_copy(freq_hbm, freqb, sem.at[6]))
 
     barrier = pltpu.get_barrier_semaphore()
     greet = [{"tp": partner}]
-    for axis in range(3):
-        for k in range(1, axes[axis][1]):
-            greet.append({"dp": peer(axis, k)})
+    for phase in range(2):
+        for k in range(1, group_size[phase]):
+            greet.append({"dp": peer(phase, k)})
     first = [lambda: [copy_x().start()], lambda: [c.start() for c in small],
              lambda: [copy_k().start()], lambda: [copy_v().start()]]
     first += [lambda c=c: [copy_q(c).start()] for c in range(3)]
@@ -169,12 +183,9 @@
         l = pltpu.roll(u, ROT_DIM // 2, 1)
         return (u * keep + r * from_right + l * from_left).astype(BF16)
 
-    copy_k().wait()
+    arrive(6, 4, 7)
     copy_up(2).start()
     copy_up(3).start()
-    copy_v().wait()
-    copy_up(4).start()
-    copy_up(5).start()
     kk = proj(6)
     vv = proj(8)
     for g in range(4):
@@ -213,99 +224,90 @@
             qs[pl.ds((4 * c + j) * ROWS, ROWS), :] = rope(qq[:, j * HEAD_DIM:(j + 1) * HEAD_DIM])
 
     head_sq = jnp.zeros((1, ROWS), F32)
-    copy_q(0).wait()
-    copy_up(6).start()
-    copy_up(7).start()
-    copy_q(1).wait()
+    arrive(0, 4, 8)
+    copy_up(4).start()
+    copy_up(5).start()
     query(0)
     query(1)
     head_sq = attention(0, head_sq)
     head_sq = attention(1, head_sq)
-    copy_q(2).wait()
-    copy_up(N_UP - 1).start()
+    arrive(4, 2, 9)
+    copy_up(6).start()
+    copy_up(7).start()
+    copy_up_half(0).start()
+    copy_up_half(1).start()
     query(2)
     head_sq = attention(2, head_sq)
     head_sq = attention(3, head_sq)
     esc[:, pl.ds(D, 128)] = head_sq
 
-    def send_o(c):
+    def send(c):
         return pltpu.make_async_remote_copy(
-            src_ref=osend.at[c], dst_ref=orecv.at[c],
-            send_sem=tp_send.at[c], recv_sem=tp_recv.at[c],
+            src_ref=xsend.at[c], dst_ref=xrecv.at[c], send_sem=tp_send, recv_sem=tp_recv.at[TP_SEM[c]],
             device_id={"tp": partner}, device_id_type=MESH)
 
-    def send_d(c):
-        return pltpu.make_async_remote_copy(
-            src_ref=dsend.at[c], dst_ref=drecv.at[c],
-            send_sem=tp_send.at[N_O + c], recv_sem=tp_recv.at[N_O + c],
-            device_id={"tp": partner}, device_id_type=MESH)
+    def receive(c, n):
+        part = pl.ds(c, n)
+        pltpu.make_async_remote_copy(
+            src_ref=xsend.at[part], dst_ref=xrecv.at[part], send_sem=tp_send, recv_sem=tp_recv.at[TP_SEM[c]],
+            device_id={"tp": partner}, device_id_type=MESH).wait_recv()
 
     pl.semaphore_wait(barrier, n_peers)
 
-    def finish_o(c):
-        send_o(c).wait_recv()
-        cs = pl.ds(c * CW, CW)
-        xm[:, cs] = (xb[:, cs].astype(F32) + (osend[c] + orecv[c])).astype(BF16)
-
     for part in range(2):
-        for c in range(3 * part, 3 * part + 3):
-            copy_o(c).wait()
+        arrive(O_U + 3 * part, 3, 10 + part)
         if part == 0:
             copy_dn(0).start()
             copy_dn(1).start()
         else:
             copy_dn(2).start()
         for c in range(3 * part, 3 * part + 3):
-            osend[c] = jnp.dot(at[...], wbuf[pl.ds((O_U + c) * UNIT, UNIT), :], preferred_element_type=F32)
-            send_o(c).start()
+            xsend[c] = jnp.dot(at[...], wbuf[pl.ds((O_U + c) * UNIT, UNIT), :], preferred_element_type=F32)
+            send(c).start()
         if part == 1:
             copy_dn(3).start()
-    for c in range(N_O):
-        finish_o(c)
+    for part in range(2):
+        receive(3 * part, 3)
+        for c in range(3 * part, 3 * part + 3):
+            cs = pl.ds(c * CW, CW)
+            xm[:, cs] = (xb[:, cs].astype(F32) + (xsend[c] + xrecv[c])).astype(BF16)
 
     esc[:, pl.ds(0, D)] = esc[:, pl.ds(0, D)] + layer_norm(xm, hb, 1)
 
-    def ar_copy(buf, group, phase, axis, k):
-        idx = axes[axis][0]
+    def ar_copy(buf, group, phase, src, k):
         return pltpu.make_async_remote_copy(
-            src_ref=buf.at[phase, idx], dst_ref=buf.at[phase, idx],
-            send_sem=ar_send.at[group, phase, k - 1], recv_sem=ar_recv.at[group, phase, k - 1],
-            device_id={"dp": peer(axis, k)}, device_id_type=MESH)
-
-    def ar_start(buf, group, phase, axis, value):
-        buf[phase, axes[axis][0]] = value
-        for k in range(1, axes[axis][1]):
-            ar_copy(buf, group, phase, axis, k).start()
-
-    def ar_finish(buf, group, phase, axis):
-        for k in range(1, axes[axis][1]):
-            ar_copy(buf, group, phase, axis, k).wait()
+            src_ref=src, dst_ref=src, send_sem=ar_send.at[group], recv_sem=ar_recv.at[group, phase],
+            device_id={"dp": peer(phase, k)}, device_id_type=MESH)
+
+    def ar_start(buf, group, phase, value):
+        buf[phase, place[phase]] = value
+        for k in range(1, group_size[phase]):
+            ar_copy(buf, group, phase, buf.at[phase, place[phase]], k).start()
+
+    def ar_finish(buf, group, phase):
+        ar_copy(buf, group, phase, buf.at[phase, pl.ds(0, group_size[phase] - 1)], 1).wait_recv()
         total = buf[phase, 0]
-        for j in range(1, axes[axis][1]):
+        for j in range(1, group_size[phase]):
             total = total + buf[phase, j]
         return total
 
-    def e_start(phase, value):
-        ar_start(are, 3, phase, phase, value)
-
-    def e_finish(phase):
-        return ar_finish(are, 3, phase, phase)
-
-    def n_step(phase):
-        for part in range(3):
-            if phase == 0:
-                value = nsc[:, pl.ds(part * PN, PN)]
-            else:
-                value = ar_finish(arn.at[part], part, phase - 1, (part + phase - 1) % 3)
-            if phase < 3:
-                ar_start(arn.at[part], part, phase, (part + phase) % 3, value)
-            else:
-                fn_ref[pl.ds(part * PN, PN)] = jnp.sqrt(value).reshape(PN)
-
-    e_start(0, esc[...])
-
-    def up_chunk(c):
-        u = jnp.dot(hb[...], wbuf[pl.ds((UP_U + 2 * c) % NU * UNIT, 2 * UNIT), :], preferred_element_type=F32)
+    def ar_sent(buf, group):
+        ar_copy(buf, group, 0, buf.at[:, pl.ds(0, group_size[0] - 1)], 1).wait_send()
+
+    def e_finish():
+        total = jnp.sqrt(ar_finish(are, 0, 1))
+        fe_ref[...] = total[:, :D].reshape(D)
+        fh_ref[...] = total[:, D:].reshape(128)[:12]
+
+    def na_finish():
+        fn_ref[pl.ds(0, NA)] = jnp.sqrt(ar_finish(arn, 1, 1)).reshape(NA)
+
+    def nb_finish():
+        fn_ref[pl.ds(NA, FL - NA)] = jnp.sqrt(ar_finish(arm, 2, 1)).reshape(FL - NA)
+
+    ar_start(are, 0, 0, esc[...])
+
+    def up_score(c, u):
         r = jnp.maximum(u, 0.0)
         a = r * r
         cs = pl.ds(c * CW, CW)
@@ -314,34 +316,41 @@
         m1 = jnp.sum(a[SEQ:], axis=0, keepdims=True) * (1.0 / SEQ)
         nsc[:, cs] = m0 * m0 + m1 * m1
 
-    for i, chunks in enumerate(((0, 1, 2), (3, 4, 5), (6, 7), (8,))):
-        for c in chunks:
-            copy_up(c).wait()
+    def up_dot(c, half, n):
+        u0 = (UP_U + 2 * c) % NU + half
+        return jnp.dot(hb[:, pl.ds(half * UNIT, n * UNIT)], wbuf[pl.ds(u0 * UNIT, n * UNIT), :],
+                       preferred_element_type=F32)
+
+    for i, chunks in enumerate(((0, 1, 2), (3, 4), (5,), (6,), (7,))):
+        arrive(UP_U + 2 * chunks[0], 2 * len(chunks), UP_SEM[chunks[0]])
         if i == 1:
             copy_dn(4).start()
             copy_dn(5, 0, 1).start()
-        elif i >= 2:
-            copy_dn(5, i - 1, 1).start()
+        elif i == 3:
+            copy_dn(5, 1, 1).start()
+            copy_dn(5, 2, 1).start()
         for c in chunks:
-            up_chunk(c)
-    n_step(0)
-    e_start(1, e_finish(0))
-
-    def finish_d(c):
-        send_d(c).wait_recv()
-        cs = pl.ds(c * CW, CW)
-        y_ref[:, cs] = (xm[:, cs].astype(F32) + (dsend[c] + drecv[c])).astype(BF16)
-
-    def finish_e():
-        total = jnp.sqrt(e_finish(2))
-        fe_ref[...] = total[:, :D].reshape(D)
-        fh_ref[...] = total[:, D:].reshape(128)[:12]
+            up_score(c, up_dot(c, 0, 2))
+        if i == 2:
+            ar_start(arn, 1, 0, nsc[:, pl.ds(0, NA)])
+    last = N_UP - 1
+    copy_up_half(0).wait()
+    u = up_dot(last, 0, 1)
+    copy_up_half(1).wait()
+    up_score(last, u + up_dot(last, 1, 1))
+    ar_start(arm, 2, 0, nsc[:, pl.ds(NA, FL - NA)])
+
+    def finish_d(first, n):
+        receive(N_O + first, n)
+        for c in range(first, first + n):
+            cs = pl.ds(c * CW, CW)
+            y_ref[:, cs] = (xm[:, cs].astype(F32) + (xsend[N_O + c] + xrecv[N_O + c])).astype(BF16)
 
     hooks = {
-        1: lambda: n_step(1),
-        2: lambda: e_start(2, e_finish(1)),
-        3: lambda: n_step(2),
-        4: finish_e,
+        0: lambda: ar_start(are, 0, 1, ar_finish(are, 0, 0)),
+        1: lambda: ar_start(arn, 1, 1, ar_finish(arn, 1, 0)),
+        2: lambda: ar_start(arm, 2, 1, ar_finish(arm, 2, 0)),
+        5: lambda: (e_finish(), na_finish()),
     }
 
     for c in range(N_DN):
@@ -353,20 +362,22 @@
                            wbuf[pl.ds((DN_B + DN_U * c + u) * UNIT, n * UNIT), :],
                            preferred_element_type=F32)
             acc = part if acc is None else acc + part
-        dsend[c] = acc
-        send_d(c).start()
-        if c >= 2:
-            finish_d(c - 2)
+        xsend[N_O + c] = acc
+        send(N_O + c).start()
+        if c in (3, 5):
+            finish_d(c - 3, 2)
         if c in hooks:
             hooks[c]()
-    finish_d(N_DN - 2)
-    finish_d(N_DN - 1)
-    n_step(3)
-
-    for c in range(N_O):
-        send_o(c).wait_send()
-    for c in range(N_DN):
-        send_d(c).wait_send()
+    finish_d(N_DN - 2, 1)
+    finish_d(N_DN - 1, 1)
+    nb_finish()
+
+    pltpu.make_async_remote_copy(
+        src_ref=xsend, dst_ref=xrecv, send_sem=tp_send, recv_sem=tp_recv.at[0],
+        device_id={"tp": partner}, device_id_type=MESH).wait_send()
+    ar_sent(are, 0)
+    ar_sent(arn, 1)
+    ar_sent(arm, 2)
 
 
 def writer(y, fn, fh, fe, y_out, fn_out, fh_out, fe_out, sem):
@@ -410,21 +421,18 @@
                 pltpu.VMEM((ROWS, KL), BF16),
                 pltpu.VMEM((ROWS, QL), BF16),
                 pltpu.VMEM((ROWS, FL), BF16),
-                pltpu.VMEM((N_O, ROWS, CW), F32),
-                pltpu.VMEM((N_O, ROWS, CW), F32),
-                pltpu.VMEM((N_DN, ROWS, CW), F32),
-                pltpu.VMEM((N_DN, ROWS, CW), F32),
+                pltpu.VMEM((N_O + N_DN, ROWS, CW), F32),
+                pltpu.VMEM((N_O + N_DN, ROWS, CW), F32),
                 pltpu.VMEM((1, FL), F32),
                 pltpu.VMEM((1, EH), F32),
-                pltpu.VMEM((3, 4, 1, EH), F32),
-                pltpu.VMEM((3, 3, 4, 1, PN), F32),
-                pltpu.SemaphoreType.DMA((20,)),
-                pltpu.SemaphoreType.DMA((N_DN + DN_U - 1,)),
-                pltpu.SemaphoreType.DMA((7,)),
-                pltpu.SemaphoreType.DMA((N_O + N_DN,)),
-                pltpu.SemaphoreType.DMA((N_O + N_DN,)),
-                pltpu.SemaphoreType.DMA((4, 3, 3)),
-                pltpu.SemaphoreType.DMA((4, 3, 3)),
+                pltpu.VMEM((2, 8, 1, EH), F32),
+                pltpu.VMEM((2, 8, 1, NA), F32),
+                pltpu.VMEM((2, 8, 1, FL - NA), F32),
+                pltpu.SemaphoreType.DMA((12,)),
+                pltpu.SemaphoreType.DMA,
+                pltpu.SemaphoreType.DMA((6,)),
+                pltpu.SemaphoreType.DMA((3,)),
+                pltpu.SemaphoreType.DMA((3, 2)),
             ],
             compiler_params=pltpu.CompilerParams(
                 collective_id=0, has_side_effects=True, vmem_limit_bytes=62 * 2**20),

time: 36.3 us -> 33 us (0.909)
  the two profiles are of different devices: /device:TPU:1 before, /device:TPU:0 now
where the time goes in v4:
time: 33 us; the launch traced here: 32.9 us
  Pallas kernels  32.2 us (98%)
  between operations  0.64 us (2%)
    pallas_call x1, Pallas kernels, local_layer(): pl.pallas_call(functools.partial(body, dims), out_shape=(pltpu.VMEM((ROWS...  31.3 us
    pallas_call x1, Pallas kernels, local_layer(): pl.pallas_call(writer, out_shape=tuple((jax.ShapeDtypeStruct(v.shape, v.d...  0.92 us

profile of v4, /device:TPU:0, one launch (start us, length us, event | category | flops | bytes accessed | tf_op | source)
XLA Modules:
  0.0 32.9 jit_solution(12655346446156001246)
XLA Ops:
  0.6 31.3 %layer.1 = (bf16[128,3072]{1,0:T(8,128)(2,1)S(1)}, f32[4608]{0:T(1024)S(1)}, f32[12]{0:T(128)S(1)}, f32[3072]{0:T(1024)S(1)}) custom-call(bf16[128,3072]{1,0:T(8,128)(2,1)} %bitcast.2, s32[64]{0:T(128)} %pos_hbm.1, f32[1,128]{1,0:T(1,128)} %constant.2.clone.freq_hbm, bf16[3072]{0:T(1024)(128)(2,1)} %g1.1, bf16[3072]{0:T(1024)(128)(2,1)} %b1.1, ...), custom_call_target="tpu_custom_call" | custom-call | tf_op jit(solution)/shard_map/layer/pallas_call | solution.py:398
  32.0 0.9 %writer.1 = (bf16[128,3072]{1,0:T(8,128)(2,1)}, f32[4608]{0:T(1024)}, f32[12]{0:T(128)}, f32[3072]{0:T(1024)}) custom-call(bf16[128,3072]{1,0:T(8,128)(2,1)S(1)} %get-tuple-element.12.y, f32[4608]{0:T(1024)S(1)} %get-tuple-element.13.fn, f32[12]{0:T(128)S(1)} %get-tuple-element.14.fh, f32[3072]{0:T(1024)S(1)} %get-tuple-element.15.fe), custom_call_target="tpu_custom_call" | custom-call | tf_op jit(solution)/shard_map/writer/pallas_call | solution.py:443

commit v5 on v4

--- a/solution.py
+++ b/solution.py
@@ -37,6 +37,7 @@
 DN_B = 2
 TP_SEM = (0, 0, 0, 1, 1, 1, 2, 2, 3, 3, 4, 5)
 UP_SEM = (0, 0, 0, 1, 1, 2, 3, 4)
+UP_LAST = ((0, 1536, 5), (1536, 768, 6), (2304, 768, 12))
 DN_SEM = (7, 8, 9, 10, 11, 0, 1, 2)
 
 
@@ -49,7 +50,7 @@
 def body(sizes, x_hbm, pos_hbm, freq_hbm, g1, b1, g2, b2, wq, wk, wv, wo, wup, wdn,
          y_ref, fn_ref, fh_ref, fe_ref,
          wbuf, ln0, ln1, ln2, ln3, posb, freqb, xb, hb, xm, qs, ks, vs, at, act, xsend, xrecv,
-         nsc, esc, are, arn, arm,
+         nsc, esc, are, arn, arm, ars, stage,
          sem, tp_send, tp_recv, ar_send, ar_recv):
     dims = sizes
     tp = lax.axis_index("tp")
@@ -64,13 +65,13 @@
         step, flip = k // 2, k % 2
         if phase == 0:
             to_x, to_z = lax.rem(ix + step, sx), iz
-            to_y = iy + 1 - 2 * lax.rem(iy, 2) if flip else iy
+            to_y = sy - 1 - iy if flip else iy
         else:
             to_x, to_z = ix, lax.rem(iz + step, sz)
-            to_y = sy - 1 - iy if flip else iy
+            to_y = iy + 1 - 2 * lax.rem(iy, 2) if flip else iy
         return to_x + sx * (to_y + sy * to_z)
 
-    place = (2 * ix + lax.rem(iy, 2), 2 * iz + lax.div(iy, 2))
+    place = (2 * ix + lax.div(iy, 2), 2 * iz + lax.rem(lax.div(iy + 1, 2), 2))
     group_size = (2 * sx, 2 * sz)
 
     def slot(u, n):
@@ -97,10 +98,9 @@
     def copy_up(c):
         return pltpu.make_async_copy(cols(wup, c), slot(UP_U + 2 * c, 2), sem.at[UP_SEM[c]])
 
-    def copy_up_half(half):
-        c = N_UP - 1
-        return pltpu.make_async_copy(wup.at[pl.ds(half * UNIT, UNIT), pl.ds(c * CW, CW)],
-                                     slot((UP_U + 2 * c) % NU + half, 1), sem.at[5 + half])
+    def copy_up_last(r0, n, i):
+        return pltpu.make_async_copy(wup.at[pl.ds(r0, n), pl.ds((N_UP - 1) * CW, CW)],
+                                     wbuf.at[pl.ds(r0, n), :], sem.at[i])
 
     def copy_dn(c, u=0, n=DN_U):
         return pltpu.make_async_copy(
@@ -120,6 +120,7 @@
     for phase in range(2):
         for k in range(1, group_size[phase]):
             greet.append({"dp": peer(phase, k)})
+            greet.append({"dp": peer(phase, k), "tp": partner})
     first = [lambda: [copy_x().start()], lambda: [c.start() for c in small],
              lambda: [copy_k().start()], lambda: [copy_v().start()]]
     first += [lambda c=c: [copy_q(c).start()] for c in range(3)]
@@ -234,8 +235,8 @@
     arrive(4, 2, 9)
     copy_up(6).start()
     copy_up(7).start()
-    copy_up_half(0).start()
-    copy_up_half(1).start()
+    for r0, n, i in UP_LAST:
+        copy_up_last(r0, n, i).start()
     query(2)
     head_sq = attention(2, head_sq)
     head_sq = attention(3, head_sq)
@@ -302,8 +303,50 @@
     def na_finish():
         fn_ref[pl.ds(0, NA)] = jnp.sqrt(ar_finish(arn, 1, 1)).reshape(NA)
 
+    NB = FL - NA
+
+    def cross_copy(phase, src, dst, k):
+        return pltpu.make_async_remote_copy(
+            src_ref=src, dst_ref=dst, send_sem=ar_send.at[3], recv_sem=ar_recv.at[3, phase],
+            device_id={"dp": peer(phase, k) if k else dp, "tp": partner}, device_id_type=MESH)
+
+    def cross_start(phase, src):
+        for k in range(group_size[phase]):
+            cross_copy(phase, src, ars.at[phase, place[phase]], k).start()
+
+    def cross_finish(phase):
+        cross_copy(phase, ars.at[phase], ars.at[phase], 0).wait_recv()
+        total = ars[phase, 0]
+        for j in range(1, group_size[phase]):
+            total = total + ars[phase, j]
+        return total
+
+    def nb_start():
+        @pl.when(tp == 0)
+        def _():
+            cross_start(0, nsc.at[:, pl.ds(NA, NB)])
+
+        @pl.when(tp == 1)
+        def _():
+            ar_start(arm, 2, 0, nsc[:, pl.ds(NA, NB)])
+
+    def nb_middle():
+        @pl.when(tp == 1)
+        def _():
+            stage[...] = cross_finish(0)
+            cross_start(1, stage)
+            ar_start(arm, 2, 1, ar_finish(arm, 2, 0))
+
     def nb_finish():
-        fn_ref[pl.ds(NA, FL - NA)] = jnp.sqrt(ar_finish(arm, 2, 1)).reshape(FL - NA)
+        @pl.when(tp == 0)
+        def _():
+            fn_ref[pl.ds(NA, NB)] = jnp.sqrt(cross_finish(1)).reshape(NB)
+
+        @pl.when(tp == 1)
+        def _():
+            fn_ref[pl.ds(NA, NB)] = jnp.sqrt(ar_finish(arm, 2, 1)).reshape(NB)
+            ar_sent(arm, 2)
+        cross_copy(0, ars.at[0], ars.at[0], 0).wait_send()
 
     ar_start(are, 0, 0, esc[...])
 
@@ -316,10 +359,8 @@
         m1 = jnp.sum(a[SEQ:], axis=0, keepdims=True) * (1.0 / SEQ)
         nsc[:, cs] = m0 * m0 + m1 * m1
 
-    def up_dot(c, half, n):
-        u0 = (UP_U + 2 * c) % NU + half
-        return jnp.dot(hb[:, pl.ds(half * UNIT, n * UNIT)], wbuf[pl.ds(u0 * UNIT, n * UNIT), :],
-                       preferred_element_type=F32)
+    def up_dot(c):
+        return jnp.dot(hb[...], wbuf[pl.ds((UP_U + 2 * c) * UNIT, 2 * UNIT), :], preferred_element_type=F32)
 
     for i, chunks in enumerate(((0, 1, 2), (3, 4), (5,), (6,), (7,))):
         arrive(UP_U + 2 * chunks[0], 2 * len(chunks), UP_SEM[chunks[0]])
@@ -330,15 +371,16 @@
             copy_dn(5, 1, 1).start()
             copy_dn(5, 2, 1).start()
         for c in chunks:
-            up_score(c, up_dot(c, 0, 2))
+            up_score(c, up_dot(c))
         if i == 2:
             ar_start(arn, 1, 0, nsc[:, pl.ds(0, NA)])
-    last = N_UP - 1
-    copy_up_half(0).wait()
-    u = up_dot(last, 0, 1)
-    copy_up_half(1).wait()
-    up_score(last, u + up_dot(last, 1, 1))
-    ar_start(arm, 2, 0, nsc[:, pl.ds(NA, FL - NA)])
+    u = None
+    for r0, n, i in UP_LAST:
+        copy_up_last(r0, n, i).wait()
+        part = jnp.dot(hb[:, pl.ds(r0, n)], wbuf[pl.ds(r0, n), :], preferred_element_type=F32)
+        u = part if u is None else u + part
+    up_score(N_UP - 1, u)
+    nb_start()
 
     def finish_d(first, n):
         receive(N_O + first, n)
@@ -349,7 +391,7 @@
     hooks = {
         0: lambda: ar_start(are, 0, 1, ar_finish(are, 0, 0)),
         1: lambda: ar_start(arn, 1, 1, ar_finish(arn, 1, 0)),
-        2: lambda: ar_start(arm, 2, 1, ar_finish(arm, 2, 0)),
+        2: nb_middle,
         5: lambda: (e_finish(), na_finish()),
     }
 
@@ -377,7 +419,6 @@
         device_id={"tp": partner}, device_id_type=MESH).wait_send()
     ar_sent(are, 0)
     ar_sent(arn, 1)
-    ar_sent(arm, 2)
 
 
 def writer(y, fn, fh, fe, y_out, fn_out, fh_out, fe_out, sem):
@@ -428,11 +469,13 @@
                 pltpu.VMEM((2, 8, 1, EH), F32),
                 pltpu.VMEM((2, 8, 1, NA), F32),
                 pltpu.VMEM((2, 8, 1, FL - NA), F32),
-                pltpu.SemaphoreType.DMA((12,)),
+                pltpu.VMEM((2, 8, 1, FL - NA), F32),
+                pltpu.VMEM((1, FL - NA), F32),
+                pltpu.SemaphoreType.DMA((13,)),
                 pltpu.SemaphoreType.DMA,
                 pltpu.SemaphoreType.DMA((6,)),
-                pltpu.SemaphoreType.DMA((3,)),
-                pltpu.SemaphoreType.DMA((3, 2)),
+                pltpu.SemaphoreType.DMA((4,)),
+                pltpu.SemaphoreType.DMA((4, 2)),
             ],
             compiler_params=pltpu.CompilerParams(
                 collective_id=0, has_side_effects=True, vmem_limit_bytes=62 * 2**20),

time: 33 us -> 32.9 us (level)
  the two profiles are of different devices: /device:TPU:0 before, /device:TPU:1 now
where the time goes in v5:
time: 32.9 us; the launch traced here: 32.8 us
  Pallas kernels  32 us (97%)
  between operations  0.8 us (2%)
    pallas_call x1, Pallas kernels, local_layer(): pl.pallas_call(functools.partial(body, dims), out_shape=(pltpu.VMEM((ROWS...  31.1 us
    pallas_call x1, Pallas kernels, local_layer(): pl.pallas_call(writer, out_shape=tuple((jax.ShapeDtypeStruct(v.shape, v.d...  0.92 us

profile of v5, /device:TPU:1, one launch (start us, length us, event | category | flops | bytes accessed | tf_op | source)
XLA Modules:
  0.0 32.8 jit_solution(407942428900352136)
XLA Ops:
  0.6 31.1 %layer.1 = (bf16[128,3072]{1,0:T(8,128)(2,1)S(1)}, f32[4608]{0:T(1024)S(1)}, f32[12]{0:T(128)S(1)}, f32[3072]{0:T(1024)S(1)}) custom-call(bf16[128,3072]{1,0:T(8,128)(2,1)} %bitcast.2, s32[64]{0:T(128)} %pos_hbm.1, f32[1,128]{1,0:T(1,128)} %constant.2.clone.freq_hbm, bf16[3072]{0:T(1024)(128)(2,1)} %g1.1, bf16[3072]{0:T(1024)(128)(2,1)} %b1.1, ...), custom_call_target="tpu_custom_call" | custom-call | tf_op jit(solution)/shard_map/layer/pallas_call | solution.py:439
  31.7 0.9 %writer.1 = (bf16[128,3072]{1,0:T(8,128)(2,1)}, f32[4608]{0:T(1024)}, f32[12]{0:T(128)}, f32[3072]{0:T(1024)}) custom-call(bf16[128,3072]{1,0:T(8,128)(2,1)S(1)} %get-tuple-element.12.y, f32[4608]{0:T(1024)S(1)} %get-tuple-element.13.fn, f32[12]{0:T(128)S(1)} %get-tuple-element.14.fh, f32[3072]{0:T(1024)S(1)} %get-tuple-element.15.fe), custom_call_target="tpu_custom_call" | custom-call | tf_op jit(solution)/shard_map/writer/pallas_call | solution.py:486

commit v6 on v5

--- a/solution.py
+++ b/solution.py
@@ -37,7 +37,7 @@
 DN_B = 2
 TP_SEM = (0, 0, 0, 1, 1, 1, 2, 2, 3, 3, 4, 5)
 UP_SEM = (0, 0, 0, 1, 1, 2, 3, 4)
-UP_LAST = ((0, 1536, 5), (1536, 768, 6), (2304, 768, 12))
+UP_LAST = ((0, 2304, 5), (2304, 768, 6))
 DN_SEM = (7, 8, 9, 10, 11, 0, 1, 2)
 
 
@@ -333,9 +333,9 @@
     def nb_middle():
         @pl.when(tp == 1)
         def _():
+            ar_start(arm, 2, 1, ar_finish(arm, 2, 0))
             stage[...] = cross_finish(0)
             cross_start(1, stage)
-            ar_start(arm, 2, 1, ar_finish(arm, 2, 0))
 
     def nb_finish():
         @pl.when(tp == 0)
@@ -471,7 +471,7 @@
                 pltpu.VMEM((2, 8, 1, FL - NA), F32),
                 pltpu.VMEM((2, 8, 1, FL - NA), F32),
                 pltpu.VMEM((1, FL - NA), F32),
-                pltpu.SemaphoreType.DMA((13,)),
+                pltpu.SemaphoreType.DMA((12,)),
                 pltpu.SemaphoreType.DMA,
                 pltpu.SemaphoreType.DMA((6,)),
                 pltpu.SemaphoreType.DMA((4,)),

time: 32.9 us -> 32.4 us (0.985)
  Pallas kernels: 32 us -> 31.5 us
    pallas_call x1, Pallas kernels: 31.1 us -> 30.6 us  [local_layer(): pl.pallas_call(functools.partial(body, dims), out_shape=(pltpu.VMEM((ROWS...]
where the time goes in v6:
time: 32.4 us; the launch traced here: 32.3 us
  Pallas kernels  31.5 us (97%)
  between operations  0.8 us (2%)
    pallas_call x1, Pallas kernels, local_layer(): pl.pallas_call(functools.partial(body, dims), out_shape=(pltpu.VMEM((ROWS...  30.6 us
    pallas_call x1, Pallas kernels, local_layer(): pl.pallas_call(writer, out_shape=tuple((jax.ShapeDtypeStruct(v.shape, v.d...  0.92 us

profile of v6, /device:TPU:1, one launch (start us, length us, event | category | flops | bytes accessed | tf_op | source)
XLA Modules:
  0.0 32.3 jit_solution(17827722199953333169)
XLA Ops:
  0.6 30.6 %layer.1 = (bf16[128,3072]{1,0:T(8,128)(2,1)S(1)}, f32[4608]{0:T(1024)S(1)}, f32[12]{0:T(128)S(1)}, f32[3072]{0:T(1024)S(1)}) custom-call(bf16[128,3072]{1,0:T(8,128)(2,1)} %bitcast.2, s32[64]{0:T(128)} %pos_hbm.1, f32[1,128]{1,0:T(1,128)} %constant.2.clone.freq_hbm, bf16[3072]{0:T(1024)(128)(2,1)} %g1.1, bf16[3072]{0:T(1024)(128)(2,1)} %b1.1, ...), custom_call_target="tpu_custom_call" | custom-call | tf_op jit(solution)/shard_map/layer/pallas_call | solution.py:439
  31.2 0.9 %writer.1 = (bf16[128,3072]{1,0:T(8,128)(2,1)}, f32[4608]{0:T(1024)}, f32[12]{0:T(128)}, f32[3072]{0:T(1024)}) custom-call(bf16[128,3072]{1,0:T(8,128)(2,1)S(1)} %get-tuple-element.12.y, f32[4608]{0:T(1024)S(1)} %get-tuple-element.13.fn, f32[12]{0:T(128)S(1)} %get-tuple-element.14.fh, f32[3072]{0:T(1024)S(1)} %get-tuple-element.15.fe), custom_call_target="tpu_custom_call" | custom-call | tf_op jit(solution)/shard_map/writer/pallas_call | solution.py:486

commit v7 on v6

--- a/solution.py
+++ b/solution.py
@@ -27,7 +27,7 @@
 NU = 32
 N_O = D // CW
 N_UP = FL // CW
-NA = 6 * CW
+NA = 5 * CW
 N_DN = D // CW
 DN_U = FL // UNIT
 EH = D + 128
@@ -36,8 +36,8 @@
 UP_U = 16
 DN_B = 2
 TP_SEM = (0, 0, 0, 1, 1, 1, 2, 2, 3, 3, 4, 5)
-UP_SEM = (0, 0, 0, 1, 1, 2, 3, 4)
-UP_LAST = ((0, 2304, 5), (2304, 768, 6))
+UP_SEM = (0, 0, 0, 1, 1, 2, 2, 3)
+UP_LAST = ((0, 2048, 5), (2048, 1024, 6))
 DN_SEM = (7, 8, 9, 10, 11, 0, 1, 2)
 
 
@@ -49,7 +49,7 @@
 
 def body(sizes, x_hbm, pos_hbm, freq_hbm, g1, b1, g2, b2, wq, wk, wv, wo, wup, wdn,
          y_ref, fn_ref, fh_ref, fe_ref,
-         wbuf, ln0, ln1, ln2, ln3, posb, freqb, xb, hb, xm, qs, ks, vs, at, act, xsend, xrecv,
+         wbuf, ln0, ln1, ln2, ln3, posb, freqb, xb, hb, xm, qs, ks, vs, at, act, ub, xsend, xrecv,
          nsc, esc, are, arn, arm, ars, stage,
          sem, tp_send, tp_recv, ar_send, ar_recv):
     dims = sizes
@@ -135,18 +135,20 @@
     def layer_norm(src, dst, which):
         gain = 1.0 + lnb[2 * which][...].astype(F32).reshape(1, D)
         bias = lnb[2 * which + 1][...].astype(F32).reshape(1, D)
+        for i in range(ROWS // 16):
+            rows = pl.ds(i * 16, 16)
+            v = src[rows, :].astype(F32)
+            mean = jnp.mean(v, axis=-1, keepdims=True)
+            cen = v - mean
+            var = jnp.mean(cen * cen, axis=-1, keepdims=True)
+            dst[rows, :] = (cen * lax.rsqrt(var + LN_EPS) * gain + bias).astype(BF16)
+
+    def token_squares(src):
         total = None
         for b in range(ROWS // SEQ):
             acc = None
             for i in range(SEQ // 16):
-                rows = pl.ds(b * SEQ + i * 16, 16)
-                v = src[rows, :].astype(F32)
-                mean = jnp.mean(v, axis=-1, keepdims=True)
-                cen = v - mean
-                var = jnp.mean(cen * cen, axis=-1, keepdims=True)
-                h = (cen * lax.rsqrt(var + LN_EPS) * gain + bias).astype(BF16)
-                dst[rows, :] = h
-                hf = h.astype(F32)
+                hf = src[pl.ds(b * SEQ + i * 16, 16), :].astype(F32)
                 part = hf[:8] + hf[8:]
                 acc = part if acc is None else acc + part
             mean_tok = jnp.sum(acc, axis=0, keepdims=True) * (1.0 / SEQ)
@@ -159,7 +161,7 @@
     copy_x().wait()
     copy_up(0).start()
     copy_up(1).start()
-    esc[:, pl.ds(0, D)] = layer_norm(xb, hb, 0)
+    layer_norm(xb, hb, 0)
 
     diag = (lax.broadcasted_iota(jnp.int32, (SEQ, SEQ), 0)
             == lax.broadcasted_iota(jnp.int32, (SEQ, SEQ), 1))
@@ -192,6 +194,7 @@
     for g in range(4):
         ks[pl.ds(g * ROWS, ROWS), :] = rope(kk[:, g * HEAD_DIM:(g + 1) * HEAD_DIM])
     vs[...] = vv.astype(BF16)
+    esc[:, pl.ds(0, D)] = token_squares(hb)
 
     row = lax.broadcasted_iota(jnp.int32, (3 * ROWS, ROWS), 0) & (ROWS - 1)
     col = lax.broadcasted_iota(jnp.int32, (3 * ROWS, ROWS), 1)
@@ -273,7 +276,7 @@
             cs = pl.ds(c * CW, CW)
             xm[:, cs] = (xb[:, cs].astype(F32) + (xsend[c] + xrecv[c])).astype(BF16)
 
-    esc[:, pl.ds(0, D)] = esc[:, pl.ds(0, D)] + layer_norm(xm, hb, 1)
+    layer_norm(xm, hb, 1)
 
     def ar_copy(buf, group, phase, src, k):
         return pltpu.make_async_remote_copy(
@@ -348,7 +351,6 @@
             ar_sent(arm, 2)
         cross_copy(0, ars.at[0], ars.at[0], 0).wait_send()
 
-    ar_start(are, 0, 0, esc[...])
 
     def up_score(c, u):
         r = jnp.maximum(u, 0.0)
@@ -362,7 +364,7 @@
     def up_dot(c):
         return jnp.dot(hb[...], wbuf[pl.ds((UP_U + 2 * c) * UNIT, 2 * UNIT), :], preferred_element_type=F32)
 
-    for i, chunks in enumerate(((0, 1, 2), (3, 4), (5,), (6,), (7,))):
+    for i, chunks in enumerate(((0, 1, 2), (3, 4), (5, 6), (7,))):
         arrive(UP_U + 2 * chunks[0], 2 * len(chunks), UP_SEM[chunks[0]])
         if i == 1:
             copy_dn(4).start()
@@ -371,15 +373,23 @@
             copy_dn(5, 1, 1).start()
             copy_dn(5, 2, 1).start()
         for c in chunks:
-            up_score(c, up_dot(c))
-        if i == 2:
+            ub[c % 2] = up_dot(c)
+            if c not in (0, 5):
+                up_score(c - 1, ub[(c - 1) % 2])
+        if i == 0:
+            esc[:, pl.ds(0, D)] = esc[:, pl.ds(0, D)] + token_squares(hb)
+            ar_start(are, 0, 0, esc[...])
+        if i == 1:
+            up_score(4, ub[0])
             ar_start(arn, 1, 0, nsc[:, pl.ds(0, NA)])
-    u = None
     for r0, n, i in UP_LAST:
         copy_up_last(r0, n, i).wait()
         part = jnp.dot(hb[:, pl.ds(r0, n)], wbuf[pl.ds(r0, n), :], preferred_element_type=F32)
-        u = part if u is None else u + part
-    up_score(N_UP - 1, u)
+        if r0 == 0:
+            ub[(N_UP - 1) % 2] = part
+            up_score(N_UP - 2, ub[(N_UP - 2) % 2])
+        else:
+            up_score(N_UP - 1, ub[(N_UP - 1) % 2] + part)
     nb_start()
 
     def finish_d(first, n):
@@ -389,8 +399,7 @@
             y_ref[:, cs] = (xm[:, cs].astype(F32) + (xsend[N_O + c] + xrecv[N_O + c])).astype(BF16)
 
     hooks = {
-        0: lambda: ar_start(are, 0, 1, ar_finish(are, 0, 0)),
-        1: lambda: ar_start(arn, 1, 1, ar_finish(arn, 1, 0)),
+        0: lambda: (ar_start(are, 0, 1, ar_finish(are, 0, 0)), ar_start(arn, 1, 1, ar_finish(arn, 1, 0))),
         2: nb_middle,
         5: lambda: (e_finish(), na_finish()),
     }
@@ -462,6 +471,7 @@
                 pltpu.VMEM((ROWS, KL), BF16),
                 pltpu.VMEM((ROWS, QL), BF16),
                 pltpu.VMEM((ROWS, FL), BF16),
+                pltpu.VMEM((2, ROWS, CW), F32),
                 pltpu.VMEM((N_O + N_DN, ROWS, CW), F32),
                 pltpu.VMEM((N_O + N_DN, ROWS, CW), F32),
                 pltpu.VMEM((1, FL), F32),

time: 32.4 us -> 32.2 us (level)
  no operation moved by 1% of the time
where the time goes in v7:
time: 32.2 us; the launch traced here: 32.1 us
  Pallas kernels  31.3 us (97%)
  between operations  0.8 us (2%)
    pallas_call x1, Pallas kernels, local_layer(): pl.pallas_call(functools.partial(body, dims), out_shape=(pltpu.VMEM((ROWS...  30.4 us
    pallas_call x1, Pallas kernels, local_layer(): pl.pallas_call(writer, out_shape=tuple((jax.ShapeDtypeStruct(v.shape, v.d...  0.92 us

profile of v7, /device:TPU:1, one launch (start us, length us, event | category | flops | bytes accessed | tf_op | source)
XLA Modules:
  0.0 32.1 jit_solution(5353410536640830749)
XLA Ops:
  0.6 30.4 %layer.1 = (bf16[128,3072]{1,0:T(8,128)(2,1)S(1)}, f32[4608]{0:T(1024)S(1)}, f32[12]{0:T(128)S(1)}, f32[3072]{0:T(1024)S(1)}) custom-call(bf16[128,3072]{1,0:T(8,128)(2,1)} %bitcast.2, s32[64]{0:T(128)} %pos_hbm.1, f32[1,128]{1,0:T(1,128)} %constant.2.clone.freq_hbm, bf16[3072]{0:T(1024)(128)(2,1)} %g1.1, bf16[3072]{0:T(1024)(128)(2,1)} %b1.1, ...), custom_call_target="tpu_custom_call" | custom-call | tf_op jit(solution)/shard_map/layer/pallas_call | solution.py:448
  31.0 0.9 %writer.1 = (bf16[128,3072]{1,0:T(8,128)(2,1)}, f32[4608]{0:T(1024)}, f32[12]{0:T(128)}, f32[3072]{0:T(1024)}) custom-call(bf16[128,3072]{1,0:T(8,128)(2,1)S(1)} %get-tuple-element.12.y, f32[4608]{0:T(1024)S(1)} %get-tuple-element.13.fn, f32[12]{0:T(128)S(1)} %get-tuple-element.14.fh, f32[3072]{0:T(1024)S(1)} %get-tuple-element.15.fe), custom_call_target="tpu_custom_call" | custom-call | tf_op jit(solution)/shard_map/writer/pallas_call | solution.py:496

commit v8 on v7

--- a/solution.py
+++ b/solution.py
@@ -121,7 +121,7 @@
         for k in range(1, group_size[phase]):
             greet.append({"dp": peer(phase, k)})
             greet.append({"dp": peer(phase, k), "tp": partner})
-    first = [lambda: [copy_x().start()], lambda: [c.start() for c in small],
+    first = [lambda: [copy_x().start()], lambda: [c.start(priority=1) for c in small],
              lambda: [copy_k().start()], lambda: [copy_v().start()]]
     first += [lambda c=c: [copy_q(c).start()] for c in range(3)]
     first += [lambda c=c: [copy_o(c).start()] for c in range(N_O)]

time: 32.2 us -> 37.8 us (1.17)
  Pallas kernels: 31.3 us -> 36.9 us
    pallas_call x1, Pallas kernels: 30.4 us -> 36 us  [local_layer(): pl.pallas_call(functools.partial(body, dims), out_shape=(pltpu.VMEM((ROWS...]
where the time goes in v8:
time: 37.8 us; the launch traced here: 37.7 us
  Pallas kernels  36.9 us (98%)
  between operations  0.8 us (2%)
    pallas_call x1, Pallas kernels, local_layer(): pl.pallas_call(functools.partial(body, dims), out_shape=(pltpu.VMEM((ROWS...  36 us
    pallas_call x1, Pallas kernels, local_layer(): pl.pallas_call(writer, out_shape=tuple((jax.ShapeDtypeStruct(v.shape, v.d...  0.92 us

profile of v8, /device:TPU:1, one launch (start us, length us, event | category | flops | bytes accessed | tf_op | source)
XLA Modules:
  0.0 37.7 jit_solution(2224040329043974931)
XLA Ops:
  0.6 36.0 %layer.1 = (bf16[128,3072]{1,0:T(8,128)(2,1)S(1)}, f32[4608]{0:T(1024)S(1)}, f32[12]{0:T(128)S(1)}, f32[3072]{0:T(1024)S(1)}) custom-call(bf16[128,3072]{1,0:T(8,128)(2,1)} %bitcast.2, s32[64]{0:T(128)} %pos_hbm.1, f32[1,128]{1,0:T(1,128)} %constant.2.clone.freq_hbm, bf16[3072]{0:T(1024)(128)(2,1)} %g1.1, bf16[3072]{0:T(1024)(128)(2,1)} %b1.1, ...), custom_call_target="tpu_custom_call" | custom-call | tf_op jit(solution)/shard_map/layer/pallas_call | solution.py:448
  36.6 0.9 %writer.1 = (bf16[128,3072]{1,0:T(8,128)(2,1)}, f32[4608]{0:T(1024)}, f32[12]{0:T(128)}, f32[3072]{0:T(1024)}) custom-call(bf16[128,3072]{1,0:T(8,128)(2,1)S(1)} %get-tuple-element.12.y, f32[4608]{0:T(1024)S(1)} %get-tuple-element.13.fn, f32[12]{0:T(128)S(1)} %get-tuple-element.14.fh, f32[3072]{0:T(1024)S(1)} %get-tuple-element.15.fe), custom_call_target="tpu_custom_call" | custom-call | tf_op jit(solution)/shard_map/writer/pallas_call | solution.py:496

commit v9 on v7

--- a/solution.py
+++ b/solution.py
@@ -122,9 +122,9 @@
             greet.append({"dp": peer(phase, k)})
             greet.append({"dp": peer(phase, k), "tp": partner})
     first = [lambda: [copy_x().start()], lambda: [c.start() for c in small],
-             lambda: [copy_k().start()], lambda: [copy_v().start()]]
-    first += [lambda c=c: [copy_q(c).start()] for c in range(3)]
-    first += [lambda c=c: [copy_o(c).start()] for c in range(N_O)]
+             lambda: [copy_k().start(priority=1)], lambda: [copy_v().start(priority=1)]]
+    first += [lambda c=c: [copy_q(c).start(priority=1)] for c in range(3)]
+    first += [lambda c=c: [copy_o(c).start(priority=1)] for c in range(N_O)]
     for i in range(max(len(first), len(greet))):
         if i < len(first):
             first[i]()
@@ -159,8 +159,8 @@
     for c in small:
         c.wait()
     copy_x().wait()
-    copy_up(0).start()
-    copy_up(1).start()
+    copy_up(0).start(priority=1)
+    copy_up(1).start(priority=1)
     layer_norm(xb, hb, 0)
 
     diag = (lax.broadcasted_iota(jnp.int32, (SEQ, SEQ), 0)
@@ -187,8 +187,8 @@
         return (u * keep + r * from_right + l * from_left).astype(BF16)
 
     arrive(6, 4, 7)
-    copy_up(2).start()
-    copy_up(3).start()
+    copy_up(2).start(priority=1)
+    copy_up(3).start(priority=1)
     kk = proj(6)
     vv = proj(8)
     for g in range(4):
@@ -229,17 +229,17 @@
 
     head_sq = jnp.zeros((1, ROWS), F32)
     arrive(0, 4, 8)
-    copy_up(4).start()
-    copy_up(5).start()
+    copy_up(4).start(priority=1)
+    copy_up(5).start(priority=1)
     query(0)
     query(1)
     head_sq = attention(0, head_sq)
     head_sq = attention(1, head_sq)
     arrive(4, 2, 9)
-    copy_up(6).start()
-    copy_up(7).start()
+    copy_up(6).start(priority=1)
+    copy_up(7).start(priority=1)
     for r0, n, i in UP_LAST:
-        copy_up_last(r0, n, i).start()
+        copy_up_last(r0, n, i).start(priority=1)
     query(2)
     head_sq = attention(2, head_sq)
     head_sq = attention(3, head_sq)
@@ -261,15 +261,15 @@
     for part in range(2):
         arrive(O_U + 3 * part, 3, 10 + part)
         if part == 0:
-            copy_dn(0).start()
-            copy_dn(1).start()
+            copy_dn(0).start(priority=1)
+            copy_dn(1).start(priority=1)
         else:
-            copy_dn(2).start()
+            copy_dn(2).start(priority=1)
         for c in range(3 * part, 3 * part + 3):
             xsend[c] = jnp.dot(at[...], wbuf[pl.ds((O_U + c) * UNIT, UNIT), :], preferred_element_type=F32)
             send(c).start()
         if part == 1:
-            copy_dn(3).start()
+            copy_dn(3).start(priority=1)
     for part in range(2):
         receive(3 * part, 3)
         for c in range(3 * part, 3 * part + 3):
@@ -367,11 +367,11 @@
     for i, chunks in enumerate(((0, 1, 2), (3, 4), (5, 6), (7,))):
         arrive(UP_U + 2 * chunks[0], 2 * len(chunks), UP_SEM[chunks[0]])
         if i == 1:
-            copy_dn(4).start()
-            copy_dn(5, 0, 1).start()
+            copy_dn(4).start(priority=1)
+            copy_dn(5, 0, 1).start(priority=1)
         elif i == 3:
-            copy_dn(5, 1, 1).start()
-            copy_dn(5, 2, 1).start()
+            copy_dn(5, 1, 1).start(priority=1)
+            copy_dn(5, 2, 1).start(priority=1)
         for c in chunks:
             ub[c % 2] = up_dot(c)
             if c not in (0, 5):

time: 32.2 us -> 32.2 us (level)
  no operation moved by 1% of the time
where the time goes in v9:
time: 32.2 us; the launch traced here: 32.1 us
  Pallas kernels  31.3 us (97%)
  between operations  0.8 us (2%)
    pallas_call x1, Pallas kernels, local_layer(): pl.pallas_call(functools.partial(body, dims), out_shape=(pltpu.VMEM((ROWS...  30.4 us
    pallas_call x1, Pallas kernels, local_layer(): pl.pallas_call(writer, out_shape=tuple((jax.ShapeDtypeStruct(v.shape, v.d...  0.92 us

profile of v9, /device:TPU:1, one launch (start us, length us, event | category | flops | bytes accessed | tf_op | source)
XLA Modules:
  0.0 32.1 jit_solution(898351708200853652)
XLA Ops:
  0.6 30.4 %layer.1 = (bf16[128,3072]{1,0:T(8,128)(2,1)S(1)}, f32[4608]{0:T(1024)S(1)}, f32[12]{0:T(128)S(1)}, f32[3072]{0:T(1024)S(1)}) custom-call(bf16[128,3072]{1,0:T(8,128)(2,1)} %bitcast.2, s32[64]{0:T(128)} %pos_hbm.1, f32[1,128]{1,0:T(1,128)} %constant.2.clone.freq_hbm, bf16[3072]{0:T(1024)(128)(2,1)} %g1.1, bf16[3072]{0:T(1024)(128)(2,1)} %b1.1, ...), custom_call_target="tpu_custom_call" | custom-call | tf_op jit(solution)/shard_map/layer/pallas_call | solution.py:448
  31.0 0.9 %writer.1 = (bf16[128,3072]{1,0:T(8,128)(2,1)}, f32[4608]{0:T(1024)}, f32[12]{0:T(128)}, f32[3072]{0:T(1024)}) custom-call(bf16[128,3072]{1,0:T(8,128)(2,1)S(1)} %get-tuple-element.12.y, f32[4608]{0:T(1024)S(1)} %get-tuple-element.13.fn, f32[12]{0:T(128)S(1)} %get-tuple-element.14.fh, f32[3072]{0:T(1024)S(1)} %get-tuple-element.15.fe), custom_call_target="tpu_custom_call" | custom-call | tf_op jit(solution)/shard_map/writer/pallas_call | solution.py:496
